TPU v7x, 32 devices: a whole 2x2x4 slice. The times are simulated.
32 devices in a mesh: dp: 2 (over x), tp: 4 (over z), sp: 4 (over y, core).
Axes of the slice: x: 2, y: 2, z: 4, core: 2. Of those that a mesh axis runs over, the one named last changes fastest.
Arguments:
- hidden: bfloat16 [128, 8192], P('dp'), parts along dimension 0
- norm_gain: float32 [8192], replicated
- w_query: bfloat16 [8192, 8192], P(None, 'tp')
- w_key: bfloat16 [8192, 1024], P(None, 'tp')
- w_value: bfloat16 [8192, 1024], P(None, 'tp')
- w_out: bfloat16 [8192, 8192], P('tp')
- k_cache: bfloat16 [128, 1024, 8, 128], P('dp', 'sp', 'tp'), parts along dimension 0
- v_cache: bfloat16 [128, 1024, 8, 128], P('dp', 'sp', 'tp'), parts along dimension 0
- positions: int32 [128], P('dp'), parts along dimension 0
Outputs:
- output 1: bfloat16 [128, 8192], P('dp'), parts along dimension 0
- output 2: bfloat16 [128, 1024, 8, 128], P('dp', 'sp', 'tp'), parts along dimension 0
- output 3: bfloat16 [128, 1024, 8, 128], P('dp', 'sp', 'tp'), parts along dimension 0
There are 2 independent parts. A program takes and returns all parts, laid end to end along the dimension named above; an argument that names none is the same for every part.
All inputs are finite; a program needn't handle non-finite values.
Results may differ from a plain program's by a relative error of at most 0.00432738.
Values sent between devices are 32-bit elements.
A program may use at most 1 GiB of HBM per device.

v0:
```python
import jax
import jax.numpy as jnp
from jax import lax
from jax.sharding import PartitionSpec as P

ROPE_BASE = 1000000.0
EPS = 1e-5
NEG_BIG = -1e30


def rotary(tensor, positions):
    half_dim = tensor.shape[-1] // 2
    inv_freq = 1.0 / (ROPE_BASE ** (jnp.arange(half_dim, dtype=jnp.float32) * 2.0 / tensor.shape[-1]))
    angles = positions.astype(jnp.float32)[:, None, None] * inv_freq[None, None, :]
    cosine = jnp.cos(angles)
    sine_val = jnp.sin(angles)
    first_half = tensor[..., :half_dim]
    second_half = tensor[..., half_dim:]
    return jnp.concatenate([first_half * cosine - second_half * sine_val, first_half * sine_val + second_half * cosine], axis=-1)


def solution(mesh):
    def local_step(hidden, norm_gain, w_query, w_key, w_value, w_out, k_cache, v_cache, positions):
        batch_size, seq_local, kv_local, head_dim = k_cache.shape
        q_local = w_query.shape[1] // head_dim
        group_size = q_local // kv_local
        resid_f32 = hidden.astype(jnp.float32)
        normed = (resid_f32 * lax.rsqrt(jnp.mean(resid_f32 * resid_f32, axis=-1, keepdims=True) + EPS) * norm_gain).astype(jnp.bfloat16)
        q_proj = jnp.dot(normed, w_query, preferred_element_type=jnp.float32).reshape(batch_size, q_local, head_dim)
        k_proj = jnp.dot(normed, w_key, preferred_element_type=jnp.float32).reshape(batch_size, kv_local, head_dim)
        v_new = jnp.dot(normed, w_value, preferred_element_type=jnp.float32).astype(jnp.bfloat16).reshape(batch_size, kv_local, head_dim)
        q_rot = rotary(q_proj, positions).astype(jnp.bfloat16).reshape(batch_size, kv_local, group_size, head_dim)
        k_new = rotary(k_proj, positions).astype(jnp.bfloat16)
        slot_pos = lax.axis_index("sp") * seq_local + jnp.arange(seq_local)
        slot_mask = (slot_pos[None, :] == positions[:, None])[:, :, None, None]
        k_updated = jnp.where(slot_mask, k_new[:, None], k_cache)
        v_updated = jnp.where(slot_mask, v_new[:, None], v_cache)
        scores = jnp.einsum("bkgd,bskd->bkgs", q_rot, k_updated, preferred_element_type=jnp.float32) * (head_dim ** -0.5)
        valid_mask = (slot_pos[None, :] <= positions[:, None])[:, None, None, :]
        scores = jnp.where(valid_mask, scores, NEG_BIG)
        local_max = jnp.max(scores, axis=-1, keepdims=True)
        exp_weights = jnp.where(valid_mask, jnp.exp(scores - local_max), 0.0)
        local_sum = jnp.sum(exp_weights, axis=-1, keepdims=True)
        local_acc = jnp.einsum("bkgs,bskd->bkgd", exp_weights.astype(jnp.bfloat16), v_updated, preferred_element_type=jnp.float32)
        block_stats = jnp.concatenate([local_acc, local_sum, local_max], axis=-1)
        gathered = lax.all_gather(block_stats, "sp")
        all_max = gathered[..., head_dim + 1:]
        global_max = jnp.max(all_max, axis=0)
        rescale = jnp.exp(all_max - global_max)
        total_sum = jnp.sum(gathered[..., head_dim:head_dim + 1] * rescale, axis=0)
        total_acc = jnp.sum(gathered[..., :head_dim] * rescale, axis=0)
        attn_out = (total_acc / total_sum).astype(jnp.bfloat16).reshape(batch_size, q_local * head_dim)
        part_proj = jnp.dot(attn_out, w_out, preferred_element_type=jnp.float32)
        proj_out = lax.psum(part_proj, "tp")
        return (resid_f32 + proj_out).astype(jnp.bfloat16), k_updated, v_updated

    cache_spec = P("dp", "sp", "tp", None)
    specs_in = (P("dp", None), P(None), P(None, "tp"), P(None, "tp"), P(None, "tp"), P("tp", None), cache_spec, cache_spec, P("dp"))
    specs_out = (P("dp", None), cache_spec, cache_spec)
    return jax.shard_map(local_step, mesh=mesh, in_specs=specs_in, out_specs=specs_out, check_vma=False)
```

profile of v0, /device:TPU:0, one launch (start us, length us, event | category | flops | bytes accessed | tf_op | source)
XLA Modules:
  0.0 234.7 jit_solution(9571410802871082479)
XLA Ops:
  7.3 1.6 fusion.4
  8.9 3.4 %fusion.32 = f32[64,256]{1,0:T(8,128)S(1)} fusion(bf16[8192,256]{1,0:T(8,128)(2,1)} %param.12, bf16[64,8192]{1,0:T(8,128)(2,1)} %param.9, f32[8192]{0:T(1024)} %param.10, f32[64]{0:T(128)S(1)} %add_rsqrt_fusion), kind=kOutput, calls=%fused_computation.52 | convolution fusion | flops 270532608 | bytes 5341440 | tf_op jit(solution)/shard_map/dot_general | solution.py:30
  12.4 3.1 %convolution_convert_fusion = bf16[64,256]{1,0:T(8,128)(2,1)S(1)} fusion(bf16[8192,256]{1,0:T(8,128)(2,1)} %param.13, bf16[64,8192]{1,0:T(8,128)(2,1)S(1)} %copy-done.1, f32[8192]{0:T(1024)S(1)} %copy-done.4, f32[64]{0:T(128)S(1)} %add_rsqrt_fusion), kind=kOutput, calls=%fused_computation.17 | convolution fusion | flops 270548992 | bytes 5308672 | tf_op jit(solution)/shard_map/dot_general | solution.py:31
  15.6 13.8 %convolution_bitcast_fusion = f32[8,8,16,128]{3,1,2,0:T(8,128)S(1)} fusion(bf16[8192,2048]{1,0:T(8,128)(2,1)} %param.11, bf16[64,8192]{1,0:T(8,128)(2,1)S(1)} %copy-done.1, f32[8192]{0:T(1024)S(1)} %copy-done.4, f32[64]{0:T(128)S(1)} %add_rsqrt_fusion), kind=kOutput, calls=%fused_computation.16 | convolution fusion | flops 2149580800 | bytes 35160320 | tf_op jit(solution)/shard_map/dot_general | solution.py:29
  30.3 25.4 %broadcast_select_fusion = (bf16[64,256,2,128]{3,2,1,0:T(2,128)(2,1)}, bf16[64,256,2,128]{3,2,1,0:T(2,128)(2,1)S(1)}) fusion(bf16[64,256,2,128]{3,2,1,0:T(2,128)(2,1)S(1)} %bitcast.24, pred[64,256]{1,0:T(8,128)(4,1)S(1)} %get-tuple-element.15, bf16[64,2,128]{2,1,0:T(2,128)(2,1)S(1)} %broadcast_in_dim.69, bf16[64,256,2,128]{3,2,1,0:T(2,128)(2,1)} %param.15, ...), kind=kLoop, calls=%fused_computation | loop fusion | flops 8388608 | bytes 33636352 | tf_op jit(solution)/shard_map/jit(_where)/select_n | solution.py:37
  55.8 2.5 %fusion.36 = (f32[64,2,8]{2,1,0:T(2,128)S(1)}, f32[64,2,8,256]{3,2,1,0:T(8,128)S(1)}) fusion(bf16[64,256,2,128]{3,2,1,0:T(2,128)(2,1)S(1)} %get-tuple-element.13, bf16[64,2,8,64]{3,2,1,0:T(8,128)(2,1)S(1)} %get-tuple-element.7, bf16[64,2,8,64]{3,2,1,0:T(8,128)(2,1)S(1)} %get-tuple-element.6, pred[64,256]{1,0:T(8,128)(4,1)S(1)} %get-tuple-element.14), kind=kOutput, calls=%fused_computation.54 | convolution fusion | flops 68418560 | bytes 9719808 | tf_op jit(solution)/shard_map/bkgd,bskd->bkgs/dot_general | solution.py:38
  58.2 1.8 copy-done
  60.0 0.5 fusion.14
  60.5 1.7 copy-done.3
  62.2 1.2 fusion
  63.4 0.8 copy.54
  64.2 0.8 copy.55
  65.1 1.2 pad_maximum_fusion
  66.5 37.0 %all-gather.3.cloned.1.call-done = f32[256,2,8,130]{3,2,1,0:T(8,128)} async-done(((f32[64,2,8,130]{3,2,1,0:T(8,128)}), f32[256,2,8,130]{3,2,1,0:T(8,128)}) %all-gather.3.cloned.1.call-update) | async-done | bytes 2129936 | tf_op jit(solution)/shard_map/all_gather | solution.py:46
  103.5 5.0 %fusion.35 = (f32[4,64,2,8,1]{4,3,2,1,0:T(8,128)}, f32[64,2,8]{2,1,0:T(2,128)S(1)}, f32[4,64,2,8,1]{4,3,2,1,0:T(8,128)}) fusion(f32[4,64,2,8,130]{4,3,2,1,0:T(8,128)} %bitcast.21), kind=kLoop, calls=%fused_computation.53 | loop fusion | flops 3072 | bytes 69632 | tf_op jit(solution)/shard_map/slice | solution.py:50
  108.5 0.2 slice.32
  108.7 2.6 %copy.69 = f32[4,64,2,8,1]{1,0,3,4,2:T(4,128)S(1)} copy(f32[4,64,2,8,1]{4,3,2,1,0:T(8,128)} %get-tuple-element.5) | data formatting | bytes 32768
  111.3 2.6 %copy.70 = f32[4,64,2,8,1]{1,0,3,4,2:T(4,128)S(1)} copy(f32[4,64,2,8,1]{4,3,2,1,0:T(8,128)} %get-tuple-element.3) | data formatting | bytes 32768
  113.9 4.6 %copy.68 = f32[4,64,2,8,128]{1,0,3,4,2:T(4,128)} copy(f32[4,64,2,8,128]{4,3,2,1,0:T(8,128)S(1)} %slice.32) | data formatting | bytes 4194304
  118.6 5.3 %multiply_reduce_fusion = f32[64,2,8,128]{0,2,3,1:T(8,128)S(1)} fusion(f32[4,64,2,8,128]{1,0,3,4,2:T(4,128)} %copy.68, f32[4,64,2,8]{1,0,3,2:T(4,128)S(1)} %get-tuple-element.11), kind=kLoop, calls=%fused_computation.6 | loop fusion | flops 917504 | bytes 2637824 | tf_op jit(solution)/shard_map/reduce_sum | solution.py:51
  124.0 0.4 copy.60
  124.5 14.9 %fusion.22 = f32[64,8192]{1,0:T(8,128)} fusion(bf16[2048,8192]{1,0:T(8,128)(2,1)} %param.14, bf16[8,8,16,128]{3,2,1,0:T(8,128)(2,1)S(1)} %bitcast.26), kind=kOutput, calls=%fused_computation.30 | convolution fusion | flops 2147483648 | bytes 35913728 | tf_op jit(solution)/shard_map/dot_general | solution.py:53
  139.4 85.8 %all-reduce.2.cloned.1.call-done = f32[64,8192]{1,0:T(8,128)} async-done(((f32[64,8192]{1,0:T(8,128)}), f32[64,8192]{1,0:T(8,128)}) %all-reduce.2.cloned.1.call-update) | async-done | bytes 2097168 | tf_op jit(solution)/shard_map/psum | solution.py:54
  225.1 2.7 %fusion.7 = bf16[64,8192]{1,0:T(8,128)(2,1)} fusion(f32[64,8192]{1,0:T(8,128)} %all-reduce.2.cloned.1.call-done, bf16[64,8192]{1,0:T(8,128)(2,1)S(1)} %copy-done.1), kind=kLoop, calls=%fused_computation.13 | loop fusion | flops 1572864 | bytes 4194304 | tf_op jit(solution)/shard_map/convert_element_type | solution.py:55
  (34 shorter events, 1.5 us)
Async XLA Ops:
  7.2 5.2 %copy-start.1 = (bf16[64,8192]{1,0:T(8,128)(2,1)S(1)}, bf16[64,8192]{1,0:T(8,128)(2,1)}, u32[]{:S(2)}) copy-start(bf16[64,8192]{1,0:T(8,128)(2,1)} %param.9) | copy-start | bytes 3145732
  7.2 5.2 %copy-start.4 = (f32[8192]{0:T(1024)S(1)}, f32[8192]{0:T(1024)}, u32[]{:S(2)}) copy-start(f32[8192]{0:T(1024)} %param.10) | copy-start | bytes 98308
  7.2 5.2 %copy-start.5 = (s32[64]{0:T(128)S(1)}, s32[64]{0:T(128)}, u32[]{:S(2)}) copy-start(s32[64]{0:T(128)} %param.17) | copy-start | bytes 772
  7.2 96.3 %all-gather.3.cloned.1.call-start = ((), (), s32[]{:S(2)}) async-start(), calls=%async_computation.1 | async-start | bytes 5242880 | tf_op jit(solution)/shard_map/all_gather | solution.py:46
  15.5 14.8 %slice-start = ((s8[8388608]{0:T(1024)(128)(4,1)}), s8[4194304]{0:T(1024)(128)(4,1)S(1)}, s32[]{:S(2)}) async-start(s8[8388608]{0:T(1024)(128)(4,1)} %bitcast.23), calls=%async_computation.2 | async-start | bytes 8388608
  15.6 14.7 %slice-start.1 = ((s8[8388608]{0:T(1024)(128)(4,1)}), s8[4194304]{0:T(1024)(128)(4,1)S(1)}, s32[]{:S(2)}) async-start(s8[8388608]{0:T(1024)(128)(4,1)} %bitcast.23), calls=%async_computation.3 | async-start | bytes 8388608
  55.8 4.3 %copy-start = (bf16[64,256,2,128]{3,2,1,0:T(2,128)(2,1)}, bf16[64,256,2,128]{3,2,1,0:T(2,128)(2,1)S(1)}, u32[]{:S(2)}) copy-start(bf16[64,256,2,128]{3,2,1,0:T(2,128)(2,1)S(1)} %get-tuple-element.13) | copy-start | bytes 25165828
  55.8 6.4 %copy-start.3 = (bf16[64,256,2,128]{3,2,1,0:T(2,128)(2,1)S(1)}, bf16[64,256,2,128]{3,2,1,0:T(2,128)(2,1)}, u32[]{:S(2)}) copy-start(bf16[64,256,2,128]{3,2,1,0:T(2,128)(2,1)} %get-tuple-element.12) | copy-start | bytes 25165828
  66.3 158.9 %all-reduce.2.cloned.1.call-start = ((), (), s32[]{:S(2)}) async-start(), calls=%async_computation | async-start | bytes 4194304 | tf_op jit(solution)/shard_map/psum | solution.py:54
  103.5 5.0 %copy-start.2 = (f32[256,2,8,130]{3,2,1,0:T(8,128)S(1)}, f32[256,2,8,130]{3,2,1,0:T(8,128)}, u32[]{:S(2)}) copy-start(f32[256,2,8,130]{3,2,1,0:T(8,128)} %all-gather.3.cloned.1.call-done) | copy-start | bytes 6389764
Sparse Core Ops, SparseCore 0:
  66.4 37.0 all-gather.2
  139.5 85.5 all-reduce.1
where the time goes:
time: 235 us
  waiting for transfers between devices  123 us (52%)
  other arithmetic  42.6 us (18%)
  matrix products  39 us (17%)
  local copies, waits for them, and re-layouts  15.8 us (7%)
  between operations  14.3 us (6%)
    psum x1, waiting for transfers between devices, local_step(): proj_out = lax.psum(part_proj, 'tp')  85.8 us
    all_gather x1, waiting for transfers between devices, local_step(): gathered = lax.all_gather(block_stats, 'sp')  37 us
    select_n x1, other arithmetic, local_step(): v_updated = jnp.where(slot_mask, v_new[:, None], v_cache)  25.4 us
    dot_general x1, matrix products, local_step(): part_proj = jnp.dot(attn_out, w_out, preferred_element_type=jnp.float32)  14.9 us
    dot_general x1, matrix products, local_step(): jnp.dot(normed, w_query, preferred_element_type=jnp.float32)  13.8 us
    unnamed x21, local copies, waits for them, and re-layouts  13.4 us
    reduce_sum x1, other arithmetic, local_step(): total_acc = jnp.sum(gathered[..., :head_dim] * rescale, axis=0)  5.28 us
    slice x1, other arithmetic, local_step(): total_sum = jnp.sum(gathered[..., head_dim:head_dim + 1] * rescale, axis=0)  4.99 us
  transfers between devices with their start and end apart: 2, of which 2 were waited for; matrix products, arithmetic and copies ran while one was open for 0% of the time, Pallas kernels for 0%

commit v1 on v0

v1 whole, which is shorter than its diff:
```python
import functools

import jax
import jax.numpy as jnp
from jax import lax
from jax.experimental import pallas as pl
from jax.experimental.pallas import tpu as pltpu
from jax.sharding import PartitionSpec as P

ROPE_BASE = 1000000.0
EPS = 1e-5
NEG_BIG = float(jnp.finfo(jnp.float32).min)
MESH = pl.DeviceIdType.MESH
F32 = jnp.float32
BF16 = jnp.bfloat16
VMEM_LIMIT = 60 * 1024 * 1024
NC = 8
NS = 4
LAG = 3


def remote(src, dst, send, recv, device):
    return pltpu.make_async_remote_copy(
        src_ref=src, dst_ref=dst, send_sem=send, recv_sem=recv, device_id=device, device_id_type=MESH
    )


def round_bf16(x):
    return x.astype(BF16).astype(F32)


def qkv_kernel(
    hid, gain, cosf, sinf, wq, wk, wv, q_out, kv_out,
    hbuf, gbuf, rbuf, wqb, wkvb, q_own, q_land, kv_own, kv_land, hsem, wsem, ssem, rsem,
):
    me = lax.axis_index("sp")
    core = lax.rem(me, 2)
    partner = {"sp": me + 1 - 2 * core}
    batch, d_model = hid.shape
    tiles, _, cols = wqb.shape
    half = tiles * cols
    hcopy = pltpu.make_async_copy(hid, hbuf, hsem.at[0])
    gcopy = pltpu.make_async_copy(gain, gbuf, hsem.at[1])
    hcopy.start()
    gcopy.start()
    head_cols = pl.ds(pl.multiple_of(core * 128, 128), 128)
    kcopy = pltpu.make_async_copy(wk.at[:, head_cols], wkvb.at[:, pl.ds(0, 128)], hsem.at[2])
    vcopy = pltpu.make_async_copy(wv.at[:, head_cols], wkvb.at[:, pl.ds(128, 128)], hsem.at[3])
    kcopy.start()
    vcopy.start()

    def wcopy(t):
        return pltpu.make_async_copy(
            wq.at[:, pl.ds(pl.multiple_of(core * half + t * cols, cols), cols)], wqb.at[t], wsem.at[t]
        )

    for t in range(tiles):
        wcopy(t).start()
    barrier = pltpu.get_barrier_semaphore()
    pl.semaphore_signal(barrier, inc=1, device_id=partner, device_id_type=MESH)

    hcopy.wait()
    gcopy.wait()

    def norm_rows(i, carry):
        rows = pl.ds(pl.multiple_of(i * 16, 16), 16)
        x = hbuf[rows, :].astype(F32)
        scale = lax.rsqrt(jnp.sum(x * x, axis=-1, keepdims=True) * (1.0 / d_model) + EPS)
        rbuf[rows, :] = (x * scale * gbuf[...]).astype(BF16)
        return carry

    lax.fori_loop(0, batch // 16, norm_rows, 0)

    def rotate(x):
        return round_bf16(x * cosf[...] + pltpu.roll(x, 64, 1) * sinf[...])

    kcopy.wait()
    vcopy.wait()
    kv = jnp.dot(rbuf[...], wkvb[...], preferred_element_type=F32)
    kv_own[0] = rotate(kv[:, :128])
    kv_own[1] = round_bf16(kv[:, 128:])
    pl.semaphore_wait(barrier, 1)
    kv_send = remote(kv_own, kv_land, ssem.at[tiles], rsem.at[tiles], partner)
    kv_send.start()

    def q_send(t):
        rows = pl.ds(pl.multiple_of(t * 2 * batch, 2 * batch), 2 * batch)
        return remote(q_own.at[rows], q_land.at[rows], ssem.at[t], rsem.at[t], partner)

    def q_tile(t, carry):
        wcopy(t).wait()
        q = jnp.dot(rbuf[...], wqb[t], preferred_element_type=F32)
        for h in range(2):
            q_own[pl.ds(pl.multiple_of((t * 2 + h) * batch, batch), batch), :] = rotate(q[:, h * 128:(h + 1) * 128])
        q_send(t).start()
        return carry

    lax.fori_loop(0, tiles, q_tile, 0)
    rows_half = q_own.shape[0]
    q_out[pl.ds(pl.multiple_of(core * rows_half, rows_half), rows_half), :] = q_own[...]
    kv_out[core] = kv_own[...]
    kv_send.wait()
    kv_out[1 - core] = kv_land[...]
    for t in range(tiles):
        q_send(t).wait()
    q_out[pl.ds(pl.multiple_of((1 - core) * rows_half, rows_half), rows_half), :] = q_land[...]


def attention_kernel(
    pos, q_ref, kv_ref, kc, vc, ko, vo, acc_ref, stat_ref, kbuf, vbuf, mbuf, lbuf, isem, osem,
):
    batch, rows, hd = kbuf.shape
    heads = acc_ref.shape[0] // batch
    groups = batch // 8
    me = lax.axis_index("sp")
    first = me * (rows // 2)

    def seqs(g):
        return pl.ds(pl.multiple_of(g * 8, 8), 8)

    def fetch(which, g):
        src, dst = ((kc, kbuf), (vc, vbuf))[which]
        return pltpu.make_async_copy(src.at[seqs(g)], dst.at[seqs(g)], isem.at[which, g])

    def store(which, g):
        src, dst = ((kbuf, ko), (vbuf, vo))[which]
        return pltpu.make_async_copy(src.at[seqs(g)], dst.at[seqs(g)], osem.at[which, g])

    for g in range(groups):
        fetch(0, g).start()
        fetch(1, g).start()

    row_iota = lax.broadcasted_iota(jnp.int32, (16, hd), 0)
    col_iota = lax.broadcasted_iota(jnp.int32, (heads, rows), 1)
    head_iota = lax.broadcasted_iota(jnp.int32, (heads, rows), 0)
    col_head = lax.rem(col_iota, 2)
    col_pos = jnp.where(col_head == head_iota // (heads // 2), first + col_iota // 2, 1 << 20)

    def group(g, carry):
        fetch(0, g).wait()
        fetch(1, g).wait()
        for i in range(8):
            b = g * 8 + i
            slot = 2 * (pos[b] - first)
            inside = jnp.logical_and(slot >= 0, slot < rows)
            base = pl.multiple_of((jnp.clip(slot, 0, rows - 1) // 16) * 16, 16)
            target = jnp.where(inside, slot - base, -100)
            for buf, which in ((kbuf, 0), (vbuf, 1)):
                old = buf[b, pl.ds(base, 16), :].astype(F32)
                new0 = kv_ref[0, which, pl.ds(b, 1), :]
                new1 = kv_ref[1, which, pl.ds(b, 1), :]
                new = jnp.where(row_iota == target, new0, jnp.where(row_iota == target + 1, new1, old))
                buf[b, pl.ds(base, 16), :] = new.astype(BF16)
        scores = []
        for i in range(8):
            b = g * 8 + i
            q = q_ref[pl.ds(b, heads, stride=batch), :].astype(BF16)
            s = lax.dot_general(q, kbuf[b], (((1,), (1,)), ((), ())), preferred_element_type=F32) * (hd ** -0.5)
            scores.append(jnp.where(col_pos <= pos[b], s, NEG_BIG))
        for i in range(8):
            b = g * 8 + i
            s = scores[i]
            top = jnp.max(s, axis=-1, keepdims=True)
            weights = jnp.where(col_pos <= pos[b], jnp.exp(s - top), 0.0)
            total = jnp.sum(weights, axis=-1, keepdims=True)
            where = pl.ds(b, heads, stride=batch)
            acc_ref[where, :] = jnp.dot(weights.astype(BF16), vbuf[b], preferred_element_type=F32)
            mbuf[where, :] = jnp.broadcast_to(top, (heads, hd))
            lbuf[where, :] = jnp.broadcast_to(total, (heads, hd))
        store(0, g).start()
        store(1, g).start()
        return carry

    lax.fori_loop(0, groups, group, 0)
    lane = lax.broadcasted_iota(jnp.int32, (batch, hd), 1)
    packed = jnp.zeros((batch, hd), F32)
    for h in range(heads):
        packed = jnp.where(lane == h, mbuf[h * batch:(h + 1) * batch, :], packed)
        packed = jnp.where(lane == heads + h, lbuf[h * batch:(h + 1) * batch, :], packed)
    stat_ref[...] = packed
    for g in range(groups):
        store(0, g).wait()
        store(1, g).wait()


def output_kernel(
    acc, stat, hid, wo, out,
    hbuf, wob, obf, acc_p, acc_c, acc_y, o_own, o_land, st_p, st_c, st_y, part, land_a, land_b, tot,
    lsem, stsem, dsem, fsem,
):
    z = lax.axis_index("tp")
    me = lax.axis_index("sp")
    core = lax.rem(me, 2)
    mate = me + 1 - 2 * core
    across = lax.rem(me + 2, 4)
    diagonal = across + 1 - 2 * core
    partner = {"sp": mate}
    ynbr = {"sp": across}
    outer = jnp.logical_or(z == 0, z == 3)
    inner = jnp.logical_not(outer)
    z_in = jnp.where(z == 0, 1, jnp.where(z == 1, 2, jnp.where(z == 2, 1, 2)))
    z_out = jnp.where(z == 1, 0, 3)
    heads, batch, hd = acc.shape
    mine = heads // 2
    cols = wob.shape[2]
    per_dev = NC * cols
    rows_s = batch // NS

    hcopy = pltpu.make_async_copy(hid, hbuf, lsem.at[NC])

    def wcopy(j):
        return pltpu.make_async_copy(
            wo.at[:, pl.ds(pl.multiple_of(me * per_dev + j * cols, cols), cols)], wob.at[j], lsem.at[j]
        )

    barrier = pltpu.get_barrier_semaphore()
    pl.semaphore_signal(barrier, inc=1, device_id=partner, device_id_type=MESH)
    pl.semaphore_signal(barrier, inc=1, device_id=ynbr, device_id_type=MESH)

    @pl.when(z > 0)
    def _():
        pl.semaphore_signal(barrier, inc=1, device_id={"tp": z - 1}, device_id_type=MESH)

    @pl.when(z < 3)
    def _():
        pl.semaphore_signal(barrier, inc=1, device_id={"tp": z + 1}, device_id_type=MESH)

    for j in range(NC):
        wcopy(j).start()
    hcopy.start()

    @pl.when(outer)
    def _():
        pl.semaphore_wait(barrier, 3)

    @pl.when(inner)
    def _():
        pl.semaphore_wait(barrier, 4)

    def part_rows(s):
        return pl.ds(s * rows_s, rows_s)

    st_send = remote(stat, st_p, stsem.at[0], stsem.at[1], partner)
    st_send.start()
    p_send = []
    for s in range(NS):
        copy = remote(
            acc.at[pl.ds((1 - core) * mine, mine), part_rows(s)], acc_p.at[:, part_rows(s)],
            dsem.at[0, s], dsem.at[1, s], partner,
        )
        copy.start()
        p_send.append(copy)

    lane = lax.broadcasted_iota(jnp.int32, (batch, hd), 1)

    def merge(a, b):
        top = jnp.maximum(a, b)
        ea = jnp.exp(a - top)
        eb = jnp.exp(b - top)
        la = pltpu.roll(a, hd - heads, 1)
        lb = pltpu.roll(b, hd - heads, 1)
        return top, ea, eb, la * ea + lb * eb

    def own_heads(x):
        return jnp.where(core == 0, x, pltpu.roll(x, hd - mine, 1))

    st_send.wait_recv()
    top, ea, eb, total = merge(own_heads(stat[...]), own_heads(st_p[...]))
    st_c[...] = jnp.where(lane < heads, top, pltpu.roll(total, heads, 1))
    sty_send = remote(st_c, st_y, stsem.at[2], stsem.at[3], ynbr)
    sty_send.start()
    y_send = []
    for s in range(NS):
        p_send[s].wait_recv()
        sl = slice(s * rows_s, (s + 1) * rows_s)
        for h in range(mine):
            acc_c[h, sl, :] = acc[core * mine + h, sl, :] * ea[sl, h:h + 1] + acc_p[h, sl, :] * eb[sl, h:h + 1]
        copy = remote(acc_c.at[:, part_rows(s)], acc_y.at[:, part_rows(s)], dsem.at[2, s], dsem.at[3, s], ynbr)
        copy.start()
        y_send.append(copy)
    sty_send.wait_recv()
    _, ea, eb, total = merge(st_c[...], st_y[...])
    o_send = []
    for s in range(NS):
        y_send[s].wait_recv()
        sl = slice(s * rows_s, (s + 1) * rows_s)
        for h in range(mine):
            o = acc_c[h, sl, :] * ea[sl, h:h + 1] + acc_y[h, sl, :] * eb[sl, h:h + 1]
            o = round_bf16(o / total[sl, h:h + 1])
            o_own[h, sl, :] = o
            obf[sl, pl.ds(pl.multiple_of((core * mine + h) * hd, hd), hd)] = o.astype(BF16)
        copy = remote(o_own.at[:, part_rows(s)], o_land.at[:, part_rows(s)], dsem.at[4, s], dsem.at[5, s], partner)
        copy.start()
        o_send.append(copy)
    for s in range(NS):
        o_send[s].wait_recv()
        sl = slice(s * rows_s, (s + 1) * rows_s)
        for h in range(mine):
            obf[sl, pl.ds(pl.multiple_of(((1 - core) * mine + h) * hd, hd), hd)] = o_land[h, sl, :].astype(BF16)

    def send_a(j):
        return remote(part.at[j], land_a.at[j], fsem.at[0, j], fsem.at[1, j], {"tp": z_in})

    def send_b(j):
        return remote(part.at[j], land_b.at[j], fsem.at[2, j], fsem.at[3, j], {"tp": z_in})

    def send_c(j):
        return remote(tot.at[me, j], tot.at[me, j], fsem.at[4, j], fsem.at[5, j], {"tp": z_out})

    def send_d(j):
        return remote(tot.at[me, j], tot.at[me, j], fsem.at[6, j], fsem.at[7, j], ynbr)

    def send_e(j):
        return remote(tot.at[me, j], tot.at[me, j], fsem.at[8, j], fsem.at[9, j], partner)

    def send_f(j):
        return remote(tot.at[across, j], tot.at[across, j], fsem.at[10, j], fsem.at[11, j], partner)

    def project(j, carry):
        wcopy(j).wait()
        part[j] = jnp.dot(obf[...], wob[j], preferred_element_type=F32)

        @pl.when(outer)
        def _():
            send_a(j).start()

        return carry

    lax.fori_loop(0, NC, project, 0)
    hcopy.wait()

    def emit(quarter, j):
        where = pl.ds(pl.multiple_of(quarter * per_dev + j * cols, cols), cols)
        out[:, where] = (hbuf[:, where].astype(F32) + tot[quarter, j]).astype(BF16)

    def share(j):
        send_d(j).start()
        send_e(j).start()
        emit(me, j)

    def collect(j):
        send_d(j).wait_recv()
        send_f(j).start()
        emit(across, j)
        send_e(j).wait_recv()
        emit(mate, j)

    def last(j):
        send_f(j).wait_recv()
        emit(diagonal, j)

    @pl.when(outer)
    def _():
        for j in range(NC + LAG):
            if j < NC:
                send_c(j).wait_recv()
                share(j)
            if j >= LAG:
                collect(j - LAG)
        for j in range(NC):
            last(j)
        for j in range(NC):
            send_a(j).wait_send()

    @pl.when(inner)
    def _():
        for j in range(NC + 2 * LAG):
            if j < NC:
                send_a(j).wait_recv()
                part[j] = part[j] + land_a[j]
                send_b(j).start()
            if LAG <= j < NC + LAG:
                k = j - LAG
                send_b(k).wait_recv()
                tot[me, k] = part[k] + land_b[k]
                send_c(k).start()
                share(k)
            if j >= 2 * LAG:
                collect(j - 2 * LAG)
        for j in range(NC):
            last(j)
        for j in range(NC):
            send_b(j).wait_send()
            send_c(j).wait_send()

    st_send.wait_send()
    sty_send.wait_send()
    for s in range(NS):
        p_send[s].wait_send()
        y_send[s].wait_send()
        o_send[s].wait_send()
    for j in range(NC):
        send_d(j).wait_send()
        send_e(j).wait_send()
        send_f(j).wait_send()


def solution(mesh):
    vmem = pl.BlockSpec(memory_space=pltpu.VMEM)
    smem = pl.BlockSpec(memory_space=pltpu.SMEM)
    hbm = pl.BlockSpec(memory_space=pl.ANY)
    dma = pltpu.SemaphoreType.DMA

    def local_step(hidden, norm_gain, w_query, w_key, w_value, w_out, k_cache, v_cache, positions):
        batch, seq_local, kv_local, hd = k_cache.shape
        d_model, q_cols = w_query.shape
        heads = q_cols // hd
        rows = seq_local * kv_local
        half_dim = hd // 2
        inv_freq = 1.0 / (ROPE_BASE ** (jnp.arange(half_dim, dtype=F32) * 2.0 / hd))
        angles = positions.astype(F32)[:, None] * inv_freq[None, :]
        cosine, sine = jnp.cos(angles), jnp.sin(angles)
        cosf = jnp.concatenate([cosine, cosine], axis=-1)
        sinf = jnp.concatenate([-sine, sine], axis=-1)

        tiles = 4
        tcols = q_cols // 2 // tiles
        half_rows = heads // 2 * batch
        q, kv = pl.pallas_call(
            qkv_kernel,
            out_shape=(
                jax.ShapeDtypeStruct((heads * batch, hd), F32),
                jax.ShapeDtypeStruct((2, 2, batch, hd), F32),
            ),
            in_specs=[hbm, hbm, vmem, vmem, hbm, hbm, hbm],
            out_specs=(vmem, vmem),
            scratch_shapes=[
                pltpu.VMEM((batch, d_model), BF16),
                pltpu.VMEM((1, d_model), F32),
                pltpu.VMEM((batch, d_model), BF16),
                pltpu.VMEM((tiles, d_model, tcols), BF16),
                pltpu.VMEM((d_model, 2 * hd), BF16),
                pltpu.VMEM((half_rows, hd), F32),
                pltpu.VMEM((half_rows, hd), F32),
                pltpu.VMEM((2, batch, hd), F32),
                pltpu.VMEM((2, batch, hd), F32),
                dma((4,)),
                dma((tiles,)),
                dma((tiles + 1,)),
                dma((tiles + 1,)),
            ],
            compiler_params=pltpu.CompilerParams(
                collective_id=0, has_side_effects=True, vmem_limit_bytes=VMEM_LIMIT
            ),
            name="qkv",
        )(hidden, norm_gain.reshape(1, d_model), cosf, sinf, w_query, w_key, w_value)

        cache3 = jax.ShapeDtypeStruct((batch, rows, hd), BF16)
        k_upd, v_upd, acc, stat = pl.pallas_call(
            attention_kernel,
            out_shape=(
                cache3, cache3,
                jax.ShapeDtypeStruct((heads * batch, hd), F32),
                jax.ShapeDtypeStruct((batch, hd), F32),
            ),
            in_specs=[smem, vmem, vmem, hbm, hbm],
            out_specs=(hbm, hbm, vmem, vmem),
            scratch_shapes=[
                pltpu.VMEM((batch, rows, hd), BF16),
                pltpu.VMEM((batch, rows, hd), BF16),
                pltpu.VMEM((heads * batch, hd), F32),
                pltpu.VMEM((heads * batch, hd), F32),
                dma((2, batch // 8)),
                dma((2, batch // 8)),
            ],
            compiler_params=pltpu.CompilerParams(vmem_limit_bytes=VMEM_LIMIT),
            name="attention",
        )(positions, q, kv, k_cache.reshape(batch, rows, hd), v_cache.reshape(batch, rows, hd))

        mine = heads // 2
        ocols = d_model // 4 // NC
        buf = pltpu.VMEM((mine, batch, hd), F32)
        st = pltpu.VMEM((batch, hd), F32)
        chunk = pltpu.VMEM((NC, batch, ocols), F32)
        out = pl.pallas_call(
            output_kernel,
            out_shape=jax.ShapeDtypeStruct((batch, d_model), BF16),
            in_specs=[vmem, vmem, hbm, hbm],
            out_specs=vmem,
            scratch_shapes=[
                pltpu.VMEM((batch, d_model), BF16),
                pltpu.VMEM((NC, q_cols, ocols), BF16),
                pltpu.VMEM((batch, q_cols), BF16),
                buf, buf, buf, buf, buf, st, st, st, chunk, chunk, chunk,
                pltpu.VMEM((4, NC, batch, ocols), F32),
                dma((NC + 1,)),
                dma((4,)),
                dma((6, NS)),
                dma((12, NC)),
            ],
            compiler_params=pltpu.CompilerParams(
                collective_id=1, has_side_effects=True, vmem_limit_bytes=VMEM_LIMIT
            ),
            name="output",
        )(acc.reshape(heads, batch, hd), stat, hidden, w_out)
        return out, k_upd.reshape(k_cache.shape), v_upd.reshape(v_cache.shape)

    cache_spec = P("dp", "sp", "tp", None)
    specs_in = (P("dp", None), P(None), P(None, "tp"), P(None, "tp"), P(None, "tp"), P("tp", None), cache_spec, cache_spec, P("dp"))
    specs_out = (P("dp", None), cache_spec, cache_spec)
    return jax.shard_map(local_step, mesh=mesh, in_specs=specs_in, out_specs=specs_out, check_vma=False)
```

time: 235 us -> 75.7 us (0.32)
  waiting for transfers between devices: 123 us -> 0 us
  Pallas kernels: 0 us -> 71 us
  other arithmetic: 42.6 us -> 1.59 us
  matrix products: 39 us -> 0 us
  between operations: 14.3 us -> 0.66 us
  local copies, waits for them, and re-layouts: 15.8 us -> 2.26 us
    psum x1 -> x0, waiting for transfers between devices: 85.8 us -> none  [local_step(): proj_out = lax.psum(part_proj, 'tp')]
    pallas_call x0 -> x3, Pallas kernels: none -> 71 us  [the longest x1 42.9 us: local_step(): pl.pallas_call(output_kernel, out_shape=jax.ShapeDtypeStruct((batch, d_mo...]
    dot_general x6 -> x0, matrix products: 39 us -> none  [the longest x1 14.9 us: local_step(): part_proj = jnp.dot(attn_out, w_out, preferred_element_type=jnp.float32)]
    all_gather x1 -> x0, waiting for transfers between devices: 37 us -> none  [local_step(): gathered = lax.all_gather(block_stats, 'sp')]
    select_n x1 -> x0, other arithmetic: 25.4 us -> none  [local_step(): v_updated = jnp.where(slot_mask, v_new[:, None], v_cache)]
    unnamed x21 -> x1, local copies, waits for them, and re-layouts: 13.4 us -> 2.26 us
    reduce_sum x4 -> x0, other arithmetic: 7.38 us -> none  [the longest x1 5.28 us: local_step(): total_acc = jnp.sum(gathered[..., :head_dim] * rescale, axis=0)]
    slice x1 -> x0, other arithmetic: 4.99 us -> none  [local_step(): total_sum = jnp.sum(gathered[..., head_dim:head_dim + 1] * rescale, axis=0)]
  transfers between devices with their start and end apart: 2 -> 0, of which waited for: 2 -> 0; matrix products, arithmetic and copies ran while one was open for 0% -> 0% of each run, Pallas kernels for 0% -> 0%
where the time goes in v1:
time: 75.7 us; the launch traced here: 75.5 us
  Pallas kernels  71 us (94%)
  local copies, waits for them, and re-layouts  2.26 us (3%)
  other arithmetic  1.59 us (2%)
    pallas_call x1, Pallas kernels, local_step(): pl.pallas_call(output_kernel, out_shape=jax.ShapeDtypeStruct((batch, d_mo...  42.9 us
    pallas_call x1, Pallas kernels, local_step(): pl.pallas_call(attention_kernel, out_shape=(cache3, cache3, jax.ShapeDtyp...  14.3 us
    pallas_call x1, Pallas kernels, local_step(): pl.pallas_call(qkv_kernel, out_shape=(jax.ShapeDtypeStruct((heads * batch...  13.8 us
    unnamed x1, local copies, waits for them, and re-layouts  2.26 us

profile of v1, /device:TPU:0, one launch (start us, length us, event | category | flops | bytes accessed | tf_op | source)
XLA Modules:
  0.0 75.5 jit_solution(14484781465165398344)
XLA Ops:
  0.6 0.7 convert_element_type.3
  1.3 0.2 fusion
  1.5 0.7 pad_maximum_fusion
  2.2 13.8 %qkv.1 = (f32[1024,128]{1,0:T(8,128)}, f32[2,2,64,128]{3,2,1,0:T(8,128)}) custom-call(bf16[64,8192]{1,0:T(8,128)(2,1)} %hid.3, f32[1,8192]{1,0:T(1,128)} %bitcast.9, f32[64,128]{1,0:T(8,128)} %get-tuple-element.18.cosf, f32[64,128]{1,0:T(8,128)} %get-tuple-element.19.sinf, bf16[8192,2048]{1,0:T(8,128)(2,1)} %wq.1, bf16[8192,256]{1,0:T(8,128)(2,1)} %wk.1, ...), custom_call_target="tpu_custom_call" | custom-call | tf_op jit(solution)/shard_map/qkv/pallas_call | solution.py:419
  16.1 14.3 %attention.1 = (bf16[64,512,128]{2,1,0:T(8,128)(2,1)}, bf16[64,512,128]{2,1,0:T(8,128)(2,1)}, f32[1024,128]{1,0:T(8,128)}, f32[64,128]{1,0:T(8,128)}) custom-call(s32[64]{0:T(128)} %pos.1, f32[1024,128]{1,0:T(8,128)} %get-tuple-element.9.q_ref, f32[2,2,64,128]{3,2,1,0:T(8,128)} %get-tuple-element.10.kv_ref, bf16[64,512,128]{2,1,0:T(8,128)(2,1)} %bitcast.6, ...), custom_call_target="tpu_custom_call" | custom-call | tf_op jit(solution)/shard_map/attention/pallas_call | solution.py:449
  30.3 42.9 %output.1 = bf16[64,8192]{1,0:T(8,128)(2,1)} custom-call(f32[16,64,128]{2,1,0:T(8,128)} %bitcast.8, f32[64,128]{1,0:T(8,128)} %get-tuple-element.12.stat, bf16[64,8192]{1,0:T(8,128)(2,1)} %hid.3, bf16[2048,8192]{1,0:T(8,128)(2,1)} %wo.1), custom_call_target="tpu_custom_call" | custom-call | tf_op jit(solution)/shard_map/output/pallas_call | solution.py:475
  73.2 2.3 %copy.13 = bf16[64,8192]{1,0:T(8,128)(2,1)} copy(bf16[64,8192]{1,0:T(8,128)(2,1)} %output.1) | data formatting | bytes 2097152
  (1 shorter events, 0.0 us)

commit v2 on v1

--- a/solution.py
+++ b/solution.py
@@ -1,4 +1,4 @@
-import functools
+import math
 
 import jax
 import jax.numpy as jnp
@@ -13,10 +13,10 @@
 MESH = pl.DeviceIdType.MESH
 F32 = jnp.float32
 BF16 = jnp.bfloat16
-VMEM_LIMIT = 60 * 1024 * 1024
-NC = 8
+NC = 16
+WIDE = 2
 NS = 4
-LAG = 3
+LAG = 4
 
 
 def remote(src, dst, send, recv, device):
@@ -30,34 +30,61 @@
 
 
 def qkv_kernel(
-    hid, gain, cosf, sinf, wq, wk, wv, q_out, kv_out,
-    hbuf, gbuf, rbuf, wqb, wkvb, q_own, q_land, kv_own, kv_land, hsem, wsem, ssem, rsem,
+    pos, hid, gain, wq, wk, wv, kc, vc, q_out, kv_out, kc_out, vc_out,
+    pos_s, hbuf, gbuf, rbuf, wqb, wkvb, pieces, psem, hsem, wsem, csem, xsem,
 ):
     me = lax.axis_index("sp")
     core = lax.rem(me, 2)
-    partner = {"sp": me + 1 - 2 * core}
+    mate = me + 1 - 2 * core
+    across = lax.rem(me + 2, 4)
+    partner = {"sp": mate}
+    ynbr = {"sp": across}
     batch, d_model = hid.shape
     tiles, _, cols = wqb.shape
-    half = tiles * cols
+    quarter = tiles * cols
     hcopy = pltpu.make_async_copy(hid, hbuf, hsem.at[0])
     gcopy = pltpu.make_async_copy(gain, gbuf, hsem.at[1])
+    pcopy = pltpu.make_async_copy(pos, pos_s, psem.at[0])
     hcopy.start()
     gcopy.start()
+    pcopy.start()
     head_cols = pl.ds(pl.multiple_of(core * 128, 128), 128)
-    kcopy = pltpu.make_async_copy(wk.at[:, head_cols], wkvb.at[:, pl.ds(0, 128)], hsem.at[2])
-    vcopy = pltpu.make_async_copy(wv.at[:, head_cols], wkvb.at[:, pl.ds(128, 128)], hsem.at[3])
-    kcopy.start()
-    vcopy.start()
+    keys = me < 2
+
+    @pl.when(keys)
+    def _():
+        pltpu.make_async_copy(wk.at[:, head_cols], wkvb, hsem.at[2]).start()
+
+    @pl.when(jnp.logical_not(keys))
+    def _():
+        pltpu.make_async_copy(wv.at[:, head_cols], wkvb, hsem.at[2]).start()
 
     def wcopy(t):
         return pltpu.make_async_copy(
-            wq.at[:, pl.ds(pl.multiple_of(core * half + t * cols, cols), cols)], wqb.at[t], wsem.at[t]
+            wq.at[:, pl.ds(pl.multiple_of(me * quarter + t * cols, cols), cols)], wqb.at[t], wsem.at[t]
         )
 
     for t in range(tiles):
         wcopy(t).start()
     barrier = pltpu.get_barrier_semaphore()
     pl.semaphore_signal(barrier, inc=1, device_id=partner, device_id_type=MESH)
+    pl.semaphore_signal(barrier, inc=1, device_id=ynbr, device_id_type=MESH)
+
+    def cache_copy(which, g):
+        src, dst = ((kc, kc_out), (vc, vc_out))[which]
+        rows = pl.ds(g * (batch // 4), batch // 4)
+        return pltpu.make_async_copy(src.at[rows], dst.at[rows], csem.at[which, g])
+
+    pcopy.wait()
+    lane = lax.broadcasted_iota(jnp.int32, (batch, 128), 1)
+    row = lax.broadcasted_iota(jnp.int32, (batch, 128), 0)
+    position = jnp.zeros((batch, 128), jnp.int32)
+    for b in range(batch):
+        position = jnp.where(row == b, pos_s[b], position)
+    index = jnp.where(lane < 64, lane, lane - 64).astype(F32)
+    angle = position.astype(F32) * jnp.exp(index * (-2.0 / 128 * math.log(ROPE_BASE)))
+    cosf = jnp.cos(angle)
+    sinf = jnp.where(lane < 64, -1.0, 1.0) * jnp.sin(angle)
 
     hcopy.wait()
     gcopy.wait()
@@ -72,42 +99,55 @@
     lax.fori_loop(0, batch // 16, norm_rows, 0)
 
     def rotate(x):
-        return round_bf16(x * cosf[...] + pltpu.roll(x, 64, 1) * sinf[...])
-
-    kcopy.wait()
-    vcopy.wait()
+        return x * cosf + pltpu.roll(x, 64, 1) * sinf
+
+    def span(p):
+        return pl.ds(4, 1) if p == 0 else pl.ds(2 * (p - 1), 2)
+
+    def exchange(kind, owner, p, device):
+        part = pieces.at[owner, span(p)]
+        return remote(part, part, xsem.at[2 * kind, p], xsem.at[2 * kind + 1, p], device)
+
+    def publish(p):
+        exchange(0, me, p, ynbr).start()
+        exchange(1, me, p, partner).start()
+
+    pltpu.make_async_copy(wk.at[:, head_cols], wkvb, hsem.at[2]).wait()
     kv = jnp.dot(rbuf[...], wkvb[...], preferred_element_type=F32)
-    kv_own[0] = rotate(kv[:, :128])
-    kv_own[1] = round_bf16(kv[:, 128:])
-    pl.semaphore_wait(barrier, 1)
-    kv_send = remote(kv_own, kv_land, ssem.at[tiles], rsem.at[tiles], partner)
-    kv_send.start()
-
-    def q_send(t):
-        rows = pl.ds(pl.multiple_of(t * 2 * batch, 2 * batch), 2 * batch)
-        return remote(q_own.at[rows], q_land.at[rows], ssem.at[t], rsem.at[t], partner)
-
-    def q_tile(t, carry):
+    pieces[me, 4] = round_bf16(jnp.where(keys, rotate(kv), kv))
+    pl.semaphore_wait(barrier, 2)
+    publish(0)
+    for t in range(tiles):
         wcopy(t).wait()
+        if t == tiles - 1:
+            for g in range(4):
+                cache_copy(0, g).start()
+                cache_copy(1, g).start()
         q = jnp.dot(rbuf[...], wqb[t], preferred_element_type=F32)
         for h in range(2):
-            q_own[pl.ds(pl.multiple_of((t * 2 + h) * batch, batch), batch), :] = rotate(q[:, h * 128:(h + 1) * 128])
-        q_send(t).start()
-        return carry
-
-    lax.fori_loop(0, tiles, q_tile, 0)
-    rows_half = q_own.shape[0]
-    q_out[pl.ds(pl.multiple_of(core * rows_half, rows_half), rows_half), :] = q_own[...]
-    kv_out[core] = kv_own[...]
-    kv_send.wait()
-    kv_out[1 - core] = kv_land[...]
-    for t in range(tiles):
-        q_send(t).wait()
-    q_out[pl.ds(pl.multiple_of((1 - core) * rows_half, rows_half), rows_half), :] = q_land[...]
+            pieces[me, 2 * t + h] = round_bf16(rotate(q[:, h * 128:(h + 1) * 128]))
+        publish(t + 1)
+    for p in range(tiles + 1):
+        exchange(0, me, p, ynbr).wait_recv()
+        exchange(2, across, p, partner).start()
+    for p in range(tiles + 1):
+        exchange(1, me, p, partner).wait_recv()
+        exchange(2, across, p, partner).wait_recv()
+    for owner in range(4):
+        for h in range(4):
+            q_out[pl.ds((owner * 4 + h) * batch, batch), :] = pieces[owner, h]
+        kv_out[owner % 2, owner // 2] = pieces[owner, 4]
+    for p in range(tiles + 1):
+        exchange(0, me, p, ynbr).wait_send()
+        exchange(1, me, p, partner).wait_send()
+        exchange(2, across, p, partner).wait_send()
+    for g in range(4):
+        cache_copy(0, g).wait()
+        cache_copy(1, g).wait()
 
 
 def attention_kernel(
-    pos, q_ref, kv_ref, kc, vc, ko, vo, acc_ref, stat_ref, kbuf, vbuf, mbuf, lbuf, isem, osem,
+    pos, q_ref, kv_ref, kc, vc, ko, vo, acc_ref, stat_ref, kbuf, vbuf, mbuf, lbuf, osem,
 ):
     batch, rows, hd = kbuf.shape
     heads = acc_ref.shape[0] // batch
@@ -118,17 +158,9 @@
     def seqs(g):
         return pl.ds(pl.multiple_of(g * 8, 8), 8)
 
-    def fetch(which, g):
-        src, dst = ((kc, kbuf), (vc, vbuf))[which]
-        return pltpu.make_async_copy(src.at[seqs(g)], dst.at[seqs(g)], isem.at[which, g])
-
     def store(which, g):
         src, dst = ((kbuf, ko), (vbuf, vo))[which]
         return pltpu.make_async_copy(src.at[seqs(g)], dst.at[seqs(g)], osem.at[which, g])
-
-    for g in range(groups):
-        fetch(0, g).start()
-        fetch(1, g).start()
 
     row_iota = lax.broadcasted_iota(jnp.int32, (16, hd), 0)
     col_iota = lax.broadcasted_iota(jnp.int32, (heads, rows), 1)
@@ -137,8 +169,6 @@
     col_pos = jnp.where(col_head == head_iota // (heads // 2), first + col_iota // 2, 1 << 20)
 
     def group(g, carry):
-        fetch(0, g).wait()
-        fetch(1, g).wait()
         for i in range(8):
             b = g * 8 + i
             slot = 2 * (pos[b] - first)
@@ -202,15 +232,16 @@
     z_out = jnp.where(z == 1, 0, 3)
     heads, batch, hd = acc.shape
     mine = heads // 2
-    cols = wob.shape[2]
+    tile = wob.shape[2]
+    cols = tile // WIDE
     per_dev = NC * cols
     rows_s = batch // NS
 
-    hcopy = pltpu.make_async_copy(hid, hbuf, lsem.at[NC])
+    hcopy = pltpu.make_async_copy(hid, hbuf, lsem.at[NC // WIDE])
 
     def wcopy(j):
         return pltpu.make_async_copy(
-            wo.at[:, pl.ds(pl.multiple_of(me * per_dev + j * cols, cols), cols)], wob.at[j], lsem.at[j]
+            wo.at[:, pl.ds(pl.multiple_of(me * per_dev + j * tile, tile), tile)], wob.at[j], lsem.at[j]
         )
 
     barrier = pltpu.get_barrier_semaphore()
@@ -225,7 +256,7 @@
     def _():
         pl.semaphore_signal(barrier, inc=1, device_id={"tp": z + 1}, device_id_type=MESH)
 
-    for j in range(NC):
+    for j in range(NC // WIDE):
         wcopy(j).start()
     hcopy.start()
 
@@ -318,15 +349,18 @@
 
     def project(j, carry):
         wcopy(j).wait()
-        part[j] = jnp.dot(obf[...], wob[j], preferred_element_type=F32)
+        product = jnp.dot(obf[...], wob[j], preferred_element_type=F32)
+        for w in range(WIDE):
+            part[j * WIDE + w] = product[:, w * cols:(w + 1) * cols]
 
         @pl.when(outer)
         def _():
-            send_a(j).start()
+            for w in range(WIDE):
+                send_a(j * WIDE + w).start()
 
         return carry
 
-    lax.fori_loop(0, NC, project, 0)
+    lax.fori_loop(0, NC // WIDE, project, 0)
     hcopy.wait()
 
     def emit(quarter, j):
@@ -398,74 +432,73 @@
 def solution(mesh):
     vmem = pl.BlockSpec(memory_space=pltpu.VMEM)
     smem = pl.BlockSpec(memory_space=pltpu.SMEM)
-    hbm = pl.BlockSpec(memory_space=pl.ANY)
+    hbm = pl.BlockSpec(memory_space=pltpu.HBM)
     dma = pltpu.SemaphoreType.DMA
+
+    def keep(x):
+        return pltpu.with_memory_space_constraint(x, pltpu.VMEM)
+
+    def stay(x):
+        return pltpu.with_memory_space_constraint(x, pltpu.HBM)
+
+    def params(mib, collective=None):
+        if collective is None:
+            return pltpu.CompilerParams(vmem_limit_bytes=mib * 2**20)
+        return pltpu.CompilerParams(vmem_limit_bytes=mib * 2**20, collective_id=collective, has_side_effects=True)
 
     def local_step(hidden, norm_gain, w_query, w_key, w_value, w_out, k_cache, v_cache, positions):
         batch, seq_local, kv_local, hd = k_cache.shape
         d_model, q_cols = w_query.shape
         heads = q_cols // hd
         rows = seq_local * kv_local
-        half_dim = hd // 2
-        inv_freq = 1.0 / (ROPE_BASE ** (jnp.arange(half_dim, dtype=F32) * 2.0 / hd))
-        angles = positions.astype(F32)[:, None] * inv_freq[None, :]
-        cosine, sine = jnp.cos(angles), jnp.sin(angles)
-        cosf = jnp.concatenate([cosine, cosine], axis=-1)
-        sinf = jnp.concatenate([-sine, sine], axis=-1)
-
-        tiles = 4
-        tcols = q_cols // 2 // tiles
-        half_rows = heads // 2 * batch
-        q, kv = pl.pallas_call(
+        tiles = 2
+        tcols = q_cols // 4 // tiles
+        cache = (batch, rows, hd)
+        acc_type = pltpu.VMEM((heads * batch, hd), F32)
+        q, kv, k_in, v_in = pl.pallas_call(
             qkv_kernel,
-            out_shape=(
-                jax.ShapeDtypeStruct((heads * batch, hd), F32),
-                jax.ShapeDtypeStruct((2, 2, batch, hd), F32),
-            ),
-            in_specs=[hbm, hbm, vmem, vmem, hbm, hbm, hbm],
-            out_specs=(vmem, vmem),
+            out_shape=(acc_type, pltpu.VMEM((2, 2, batch, hd), F32), pltpu.VMEM(cache, BF16), pltpu.VMEM(cache, BF16)),
+            in_specs=[hbm] * 8,
+            out_specs=(vmem,) * 4,
             scratch_shapes=[
+                pltpu.SMEM((batch,), jnp.int32),
                 pltpu.VMEM((batch, d_model), BF16),
                 pltpu.VMEM((1, d_model), F32),
                 pltpu.VMEM((batch, d_model), BF16),
                 pltpu.VMEM((tiles, d_model, tcols), BF16),
-                pltpu.VMEM((d_model, 2 * hd), BF16),
-                pltpu.VMEM((half_rows, hd), F32),
-                pltpu.VMEM((half_rows, hd), F32),
-                pltpu.VMEM((2, batch, hd), F32),
-                pltpu.VMEM((2, batch, hd), F32),
-                dma((4,)),
+                pltpu.VMEM((d_model, hd), BF16),
+                pltpu.VMEM((4, 5, batch, hd), F32),
+                dma((1,)),
+                dma((3,)),
                 dma((tiles,)),
-                dma((tiles + 1,)),
-                dma((tiles + 1,)),
+                dma((2, 4)),
+                dma((6, tiles + 1)),
             ],
-            compiler_params=pltpu.CompilerParams(
-                collective_id=0, has_side_effects=True, vmem_limit_bytes=VMEM_LIMIT
-            ),
+            compiler_params=params(24, 0),
             name="qkv",
-        )(hidden, norm_gain.reshape(1, d_model), cosf, sinf, w_query, w_key, w_value)
-
-        cache3 = jax.ShapeDtypeStruct((batch, rows, hd), BF16)
-        k_upd, v_upd, acc, stat = pl.pallas_call(
+        )(
+            stay(positions), stay(hidden), stay(norm_gain.reshape(1, d_model)), stay(w_query), stay(w_key), stay(w_value),
+            stay(k_cache.reshape(cache)), stay(v_cache.reshape(cache)),
+        )
+
+        k_upd, v_upd, acc, stat, _, _ = pl.pallas_call(
             attention_kernel,
             out_shape=(
-                cache3, cache3,
-                jax.ShapeDtypeStruct((heads * batch, hd), F32),
-                jax.ShapeDtypeStruct((batch, hd), F32),
+                jax.ShapeDtypeStruct(cache, BF16), jax.ShapeDtypeStruct(cache, BF16),
+                acc_type, pltpu.VMEM((batch, hd), F32),
+                pltpu.VMEM(cache, BF16), pltpu.VMEM(cache, BF16),
             ),
-            in_specs=[smem, vmem, vmem, hbm, hbm],
-            out_specs=(hbm, hbm, vmem, vmem),
+            in_specs=[smem, vmem, vmem, vmem, vmem],
+            out_specs=(hbm, hbm, vmem, vmem, vmem, vmem),
+            input_output_aliases={3: 4, 4: 5},
             scratch_shapes=[
-                pltpu.VMEM((batch, rows, hd), BF16),
-                pltpu.VMEM((batch, rows, hd), BF16),
                 pltpu.VMEM((heads * batch, hd), F32),
                 pltpu.VMEM((heads * batch, hd), F32),
                 dma((2, batch // 8)),
-                dma((2, batch // 8)),
             ],
-            compiler_params=pltpu.CompilerParams(vmem_limit_bytes=VMEM_LIMIT),
+            compiler_params=params(10),
             name="attention",
-        )(positions, q, kv, k_cache.reshape(batch, rows, hd), v_cache.reshape(batch, rows, hd))
+        )(positions, keep(q), keep(kv), keep(k_in), keep(v_in))
 
         mine = heads // 2
         ocols = d_model // 4 // NC
@@ -474,25 +507,23 @@
         chunk = pltpu.VMEM((NC, batch, ocols), F32)
         out = pl.pallas_call(
             output_kernel,
-            out_shape=jax.ShapeDtypeStruct((batch, d_model), BF16),
+            out_shape=pltpu.VMEM((batch, d_model), BF16),
             in_specs=[vmem, vmem, hbm, hbm],
             out_specs=vmem,
             scratch_shapes=[
                 pltpu.VMEM((batch, d_model), BF16),
-                pltpu.VMEM((NC, q_cols, ocols), BF16),
+                pltpu.VMEM((NC // WIDE, q_cols, ocols * WIDE), BF16),
                 pltpu.VMEM((batch, q_cols), BF16),
                 buf, buf, buf, buf, buf, st, st, st, chunk, chunk, chunk,
                 pltpu.VMEM((4, NC, batch, ocols), F32),
-                dma((NC + 1,)),
+                dma((NC // WIDE + 1,)),
                 dma((4,)),
                 dma((6, NS)),
                 dma((12, NC)),
             ],
-            compiler_params=pltpu.CompilerParams(
-                collective_id=1, has_side_effects=True, vmem_limit_bytes=VMEM_LIMIT
-            ),
+            compiler_params=params(24, 1),
             name="output",
-        )(acc.reshape(heads, batch, hd), stat, hidden, w_out)
+        )(keep(acc.reshape(heads, batch, hd)), keep(stat), stay(hidden), stay(w_out))
         return out, k_upd.reshape(k_cache.shape), v_upd.reshape(v_cache.shape)
 
     cache_spec = P("dp", "sp", "tp", None)

time: 75.7 us -> 61 us (0.81)
  Pallas kernels: 71 us -> 59.2 us
  other arithmetic: 1.59 us -> 0 us
  local copies, waits for them, and re-layouts: 2.26 us -> 0.98 us
    pallas_call x3, Pallas kernels: 71 us -> 59.2 us  [the longest x1 38.8 us: local_step(): pl.pallas_call(output_kernel, out_shape=pltpu.VMEM((batch, d_model), BF16...]
    unnamed x1 -> x3, local copies, waits for them, and re-layouts: 2.26 us -> 0.98 us
where the time goes in v2:
time: 61 us; the launch traced here: 60.8 us
  Pallas kernels  59.2 us (97%)
  local copies, waits for them, and re-layouts  0.98 us (2%)
  between operations  0.67 us (1%)
    pallas_call x1, Pallas kernels, local_step(): pl.pallas_call(output_kernel, out_shape=pltpu.VMEM((batch, d_model), BF16...  38.8 us
    pallas_call x1, Pallas kernels, local_step(): pl.pallas_call(qkv_kernel, out_shape=(acc_type, pltpu.VMEM((2, 2, batch,...  13 us
    pallas_call x1, Pallas kernels, local_step(): pl.pallas_call(attention_kernel, out_shape=(jax.ShapeDtypeStruct(cache, B...  7.39 us

profile of v2, /device:TPU:0, one launch (start us, length us, event | category | flops | bytes accessed | tf_op | source)
XLA Modules:
  0.0 60.8 jit_solution(7218052597811224158)
XLA Ops:
  0.6 0.0 copy-start
  0.6 13.0 %qkv.1 = (f32[1024,128]{1,0:T(8,128)S(1)}, f32[2,2,64,128]{3,2,1,0:T(8,128)S(1)}, bf16[64,512,128]{2,1,0:T(8,128)(2,1)S(1)}, bf16[64,512,128]{2,1,0:T(8,128)(2,1)S(1)}) custom-call(s32[64]{0:T(128)} %pos.3, bf16[64,8192]{1,0:T(8,128)(2,1)} %hid.3, f32[1,8192]{1,0:T(1,128)} %bitcast.9, bf16[8192,2048]{1,0:T(8,128)(2,1)} %wq.1, bf16[8192,256]{1,0:T(8,128)(2,1)} %wk.1, ...), custom_call_target="tpu_custom_call" | custom-call | tf_op jit(solution)/shard_map/qkv/pallas_call | solution.py:458
  13.7 0.0 copy-done
  13.7 7.4 %attention.1 = (bf16[64,512,128]{2,1,0:T(8,128)(2,1)}, bf16[64,512,128]{2,1,0:T(8,128)(2,1)}, f32[1024,128]{1,0:T(8,128)S(1)}, f32[64,128]{1,0:T(8,128)S(1)}, bf...) custom-call(s32[64]{0:T(128)S(1)} %copy-done, ...), custom_call_target="tpu_custom_call", output_to_operand_aliasing={{4}: (3, {}), {5}: (4, {})} | custom-call | tf_op jit(solution)/shard_map/attention/pallas_call | solution.py:484
  21.1 38.8 %output.1 = bf16[64,8192]{1,0:T(8,128)(2,1)S(1)} custom-call(f32[16,64,128]{2,1,0:T(8,128)S(1)} %bitcast.6, f32[64,128]{1,0:T(8,128)S(1)} %get-tuple-element.16.stat, bf16[64,8192]{1,0:T(8,128)(2,1)} %hid.3, bf16[2048,8192]{1,0:T(8,128)(2,1)} %wo.1), custom_call_target="tpu_custom_call" | custom-call | tf_op jit(solution)/shard_map/output/pallas_call | solution.py:508
  59.9 1.0 %copy.17 = bf16[64,8192]{1,0:T(8,128)(2,1)} copy(bf16[64,8192]{1,0:T(8,128)(2,1)S(1)} %output.1) | data formatting | bytes 2097152
Async XLA Ops:
  0.6 13.0 %copy-start = (s32[64]{0:T(128)S(1)}, s32[64]{0:T(128)}, u32[]{:S(2)}) copy-start(s32[64]{0:T(128)} %pos.3) | copy-start | bytes 772

commit v3 on v2

--- a/solution.py
+++ b/solution.py
@@ -13,8 +13,10 @@
 MESH = pl.DeviceIdType.MESH
 F32 = jnp.float32
 BF16 = jnp.bfloat16
-NC = 16
-WIDE = 2
+TILES = 16
+FIRST = 6
+MOST = max(FIRST, TILES - FIRST)
+HALVES = 2
 NS = 4
 LAG = 4
 
@@ -233,16 +235,26 @@
     heads, batch, hd = acc.shape
     mine = heads // 2
     tile = wob.shape[2]
-    cols = tile // WIDE
-    per_dev = NC * cols
     rows_s = batch // NS
-
-    hcopy = pltpu.make_async_copy(hid, hbuf, lsem.at[NC // WIDE])
-
-    def wcopy(j):
-        return pltpu.make_async_copy(
-            wo.at[:, pl.ds(pl.multiple_of(me * per_dev + j * tile, tile), tile)], wob.at[j], lsem.at[j]
-        )
+    rows_h = batch // HALVES
+    mine_n = jnp.where(core == 0, FIRST, TILES - FIRST)
+    mate_n = TILES - mine_n
+
+    hcopy = pltpu.make_async_copy(hid, hbuf, lsem.at[MOST])
+
+    def columns(quarter, t):
+        first = (quarter // 2) * TILES + lax.rem(quarter, 2) * FIRST
+        return pl.ds(pl.multiple_of((first + t) * tile, tile), tile)
+
+    def wcopy(t):
+        return pltpu.make_async_copy(wo.at[:, columns(me, t)], wob.at[t], lsem.at[t])
+
+    def repeat(low, high, body):
+        def step(i, carry):
+            body(i)
+            return carry
+
+        lax.fori_loop(low, high, step, 0)
 
     barrier = pltpu.get_barrier_semaphore()
     pl.semaphore_signal(barrier, inc=1, device_id=partner, device_id_type=MESH)
@@ -256,8 +268,7 @@
     def _():
         pl.semaphore_signal(barrier, inc=1, device_id={"tp": z + 1}, device_id_type=MESH)
 
-    for j in range(NC // WIDE):
-        wcopy(j).start()
+    repeat(0, mine_n, lambda t: wcopy(t).start())
     hcopy.start()
 
     @pl.when(outer)
@@ -312,22 +323,6 @@
     sty_send.wait_recv()
     _, ea, eb, total = merge(st_c[...], st_y[...])
     o_send = []
-    for s in range(NS):
-        y_send[s].wait_recv()
-        sl = slice(s * rows_s, (s + 1) * rows_s)
-        for h in range(mine):
-            o = acc_c[h, sl, :] * ea[sl, h:h + 1] + acc_y[h, sl, :] * eb[sl, h:h + 1]
-            o = round_bf16(o / total[sl, h:h + 1])
-            o_own[h, sl, :] = o
-            obf[sl, pl.ds(pl.multiple_of((core * mine + h) * hd, hd), hd)] = o.astype(BF16)
-        copy = remote(o_own.at[:, part_rows(s)], o_land.at[:, part_rows(s)], dsem.at[4, s], dsem.at[5, s], partner)
-        copy.start()
-        o_send.append(copy)
-    for s in range(NS):
-        o_send[s].wait_recv()
-        sl = slice(s * rows_s, (s + 1) * rows_s)
-        for h in range(mine):
-            obf[sl, pl.ds(pl.multiple_of(((1 - core) * mine + h) * hd, hd), hd)] = o_land[h, sl, :].astype(BF16)
 
     def send_a(j):
         return remote(part.at[j], land_a.at[j], fsem.at[0, j], fsem.at[1, j], {"tp": z_in})
@@ -347,86 +342,130 @@
     def send_f(j):
         return remote(tot.at[across, j], tot.at[across, j], fsem.at[10, j], fsem.at[11, j], partner)
 
-    def project(j, carry):
-        wcopy(j).wait()
-        product = jnp.dot(obf[...], wob[j], preferred_element_type=F32)
-        for w in range(WIDE):
-            part[j * WIDE + w] = product[:, w * cols:(w + 1) * cols]
-
-        @pl.when(outer)
-        def _():
-            for w in range(WIDE):
-                send_a(j * WIDE + w).start()
-
-        return carry
-
-    lax.fori_loop(0, NC // WIDE, project, 0)
+    for half in range(HALVES):
+        chunks = range(half * NS // HALVES, (half + 1) * NS // HALVES)
+        for s in chunks:
+            y_send[s].wait_recv()
+            sl = slice(s * rows_s, (s + 1) * rows_s)
+            for h in range(mine):
+                o = acc_c[h, sl, :] * ea[sl, h:h + 1] + acc_y[h, sl, :] * eb[sl, h:h + 1]
+                o = round_bf16(o / total[sl, h:h + 1])
+                o_own[h, sl, :] = o
+                obf[sl, pl.ds(pl.multiple_of((core * mine + h) * hd, hd), hd)] = o.astype(BF16)
+            copy = remote(o_own.at[:, part_rows(s)], o_land.at[:, part_rows(s)], dsem.at[4, s], dsem.at[5, s], partner)
+            copy.start()
+            o_send.append(copy)
+        for s in chunks:
+            o_send[s].wait_recv()
+            sl = slice(s * rows_s, (s + 1) * rows_s)
+            for h in range(mine):
+                obf[sl, pl.ds(pl.multiple_of(((1 - core) * mine + h) * hd, hd), hd)] = o_land[h, sl, :].astype(BF16)
+
+        def project(t, half=half):
+            if half == 0:
+                wcopy(t).wait()
+            j = half * mine_n + t
+            part[j] = jnp.dot(obf[half * rows_h:(half + 1) * rows_h, :], wob[t], preferred_element_type=F32)
+
+            @pl.when(outer)
+            def _():
+                send_a(j).start()
+
+        repeat(0, mine_n, project)
     hcopy.wait()
 
-    def emit(quarter, j):
-        where = pl.ds(pl.multiple_of(quarter * per_dev + j * cols, cols), cols)
-        out[:, where] = (hbuf[:, where].astype(F32) + tot[quarter, j]).astype(BF16)
+    def emit(quarter, count, j):
+        half = j // count
+        rows = pl.ds(pl.multiple_of(half * rows_h, rows_h), rows_h)
+        where = columns(quarter, j - half * count)
+        out[rows, where] = (hbuf[rows, where].astype(F32) + tot[quarter, j]).astype(BF16)
 
     def share(j):
         send_d(j).start()
         send_e(j).start()
-        emit(me, j)
-
-    def collect(j):
+        emit(me, mine_n, j)
+
+    def collect_y(j):
         send_d(j).wait_recv()
         send_f(j).start()
-        emit(across, j)
+        emit(across, mine_n, j)
+
+    def collect_core(j):
         send_e(j).wait_recv()
-        emit(mate, j)
+        emit(mate, mate_n, j)
 
     def last(j):
         send_f(j).wait_recv()
-        emit(diagonal, j)
+        emit(diagonal, mate_n, j)
+
+    mine_c = HALVES * mine_n
+    mate_c = HALVES * mate_n
+
+    def collect(k):
+        @pl.when(k >= 0)
+        def _():
+            collect_y(k)
+
+        @pl.when(jnp.logical_and(k >= 0, k < mate_c))
+        def _():
+            collect_core(k)
 
     @pl.when(outer)
     def _():
-        for j in range(NC + LAG):
-            if j < NC:
+        def step(j):
+            @pl.when(j < mine_c)
+            def _():
                 send_c(j).wait_recv()
                 share(j)
-            if j >= LAG:
-                collect(j - LAG)
-        for j in range(NC):
-            last(j)
-        for j in range(NC):
-            send_a(j).wait_send()
+
+            collect(j - LAG)
+
+        repeat(0, mine_c + LAG, step)
+        repeat(0, mine_c, lambda j: send_a(j).wait_send())
 
     @pl.when(inner)
     def _():
-        for j in range(NC + 2 * LAG):
-            if j < NC:
+        def step(j):
+            @pl.when(j < mine_c)
+            def _():
                 send_a(j).wait_recv()
                 part[j] = part[j] + land_a[j]
                 send_b(j).start()
-            if LAG <= j < NC + LAG:
-                k = j - LAG
+
+            k = j - LAG
+
+            @pl.when(jnp.logical_and(k >= 0, k < mine_c))
+            def _():
                 send_b(k).wait_recv()
                 tot[me, k] = part[k] + land_b[k]
                 send_c(k).start()
                 share(k)
-            if j >= 2 * LAG:
-                collect(j - 2 * LAG)
-        for j in range(NC):
-            last(j)
-        for j in range(NC):
+
+            collect(j - 2 * LAG)
+
+        repeat(0, mine_c + 2 * LAG, step)
+
+        def drain(j):
             send_b(j).wait_send()
             send_c(j).wait_send()
 
+        repeat(0, mine_c, drain)
+
+    repeat(mine_c, mate_c, collect_core)
+    repeat(0, mate_c, last)
     st_send.wait_send()
     sty_send.wait_send()
     for s in range(NS):
         p_send[s].wait_send()
         y_send[s].wait_send()
         o_send[s].wait_send()
-    for j in range(NC):
+
+    def finish(j):
         send_d(j).wait_send()
         send_e(j).wait_send()
         send_f(j).wait_send()
+
+    repeat(0, mine_c, finish)
 
 
 def solution(mesh):
@@ -501,10 +540,12 @@
         )(positions, keep(q), keep(kv), keep(k_in), keep(v_in))
 
         mine = heads // 2
-        ocols = d_model // 4 // NC
+        ocols = d_model // 2 // TILES
         buf = pltpu.VMEM((mine, batch, hd), F32)
         st = pltpu.VMEM((batch, hd), F32)
-        chunk = pltpu.VMEM((NC, batch, ocols), F32)
+        messages = HALVES * MOST
+        block = (batch // HALVES, ocols)
+        chunk = pltpu.VMEM((messages,) + block, F32)
         out = pl.pallas_call(
             output_kernel,
             out_shape=pltpu.VMEM((batch, d_model), BF16),
@@ -512,16 +553,16 @@
             out_specs=vmem,
             scratch_shapes=[
                 pltpu.VMEM((batch, d_model), BF16),
-                pltpu.VMEM((NC // WIDE, q_cols, ocols * WIDE), BF16),
+                pltpu.VMEM((MOST, q_cols, ocols), BF16),
                 pltpu.VMEM((batch, q_cols), BF16),
                 buf, buf, buf, buf, buf, st, st, st, chunk, chunk, chunk,
-                pltpu.VMEM((4, NC, batch, ocols), F32),
-                dma((NC // WIDE + 1,)),
+                pltpu.VMEM((4, messages) + block, F32),
+                dma((MOST + 1,)),
                 dma((4,)),
                 dma((6, NS)),
-                dma((12, NC)),
+                dma((12, messages)),
             ],
-            compiler_params=params(24, 1),
+            compiler_params=params(28, 1),
             name="output",
         )(keep(acc.reshape(heads, batch, hd)), keep(stat), stay(hidden), stay(w_out))
         return out, k_upd.reshape(k_cache.shape), v_upd.reshape(v_cache.shape)

time: 61 us -> 62.1 us (1.018)
  Pallas kernels: 59.2 us -> 60.3 us
    pallas_call x1, Pallas kernels: 38.8 us -> 39.9 us  [local_step(): pl.pallas_call(output_kernel, out_shape=pltpu.VMEM((batch, d_model), BF16...]
where the time goes in v3:
time: 62.1 us; the launch traced here: 61.9 us
  Pallas kernels  60.3 us (97%)
  local copies, waits for them, and re-layouts  0.98 us (2%)
  between operations  0.67 us (1%)
    pallas_call x1, Pallas kernels, local_step(): pl.pallas_call(output_kernel, out_shape=pltpu.VMEM((batch, d_model), BF16...  39.9 us
    pallas_call x1, Pallas kernels, local_step(): pl.pallas_call(qkv_kernel, out_shape=(acc_type, pltpu.VMEM((2, 2, batch,...  13 us
    pallas_call x1, Pallas kernels, local_step(): pl.pallas_call(attention_kernel, out_shape=(jax.ShapeDtypeStruct(cache, B...  7.39 us

profile of v3, /device:TPU:0, one launch (start us, length us, event | category | flops | bytes accessed | tf_op | source)
XLA Modules:
  0.0 61.9 jit_solution(5855856002119740744)
XLA Ops:
  0.6 0.0 copy-start
  0.6 13.0 %qkv.1 = (f32[1024,128]{1,0:T(8,128)S(1)}, f32[2,2,64,128]{3,2,1,0:T(8,128)S(1)}, bf16[64,512,128]{2,1,0:T(8,128)(2,1)S(1)}, bf16[64,512,128]{2,1,0:T(8,128)(2,1)S(1)}) custom-call(s32[64]{0:T(128)} %pos.3, bf16[64,8192]{1,0:T(8,128)(2,1)} %hid.3, f32[1,8192]{1,0:T(1,128)} %bitcast.9, bf16[8192,2048]{1,0:T(8,128)(2,1)} %wq.1, bf16[8192,256]{1,0:T(8,128)(2,1)} %wk.1, ...), custom_call_target="tpu_custom_call" | custom-call | tf_op jit(solution)/shard_map/qkv/pallas_call | solution.py:497
  13.7 0.0 copy-done
  13.7 7.4 %attention.1 = (bf16[64,512,128]{2,1,0:T(8,128)(2,1)}, bf16[64,512,128]{2,1,0:T(8,128)(2,1)}, f32[1024,128]{1,0:T(8,128)S(1)}, f32[64,128]{1,0:T(8,128)S(1)}, bf...) custom-call(s32[64]{0:T(128)S(1)} %copy-done, ...), custom_call_target="tpu_custom_call", output_to_operand_aliasing={{4}: (3, {}), {5}: (4, {})} | custom-call | tf_op jit(solution)/shard_map/attention/pallas_call | solution.py:523
  21.1 39.9 %output.1 = bf16[64,8192]{1,0:T(8,128)(2,1)S(1)} custom-call(f32[16,64,128]{2,1,0:T(8,128)S(1)} %bitcast.6, f32[64,128]{1,0:T(8,128)S(1)} %get-tuple-element.16.stat, bf16[64,8192]{1,0:T(8,128)(2,1)} %hid.3, bf16[2048,8192]{1,0:T(8,128)(2,1)} %wo.1), custom_call_target="tpu_custom_call" | custom-call | tf_op jit(solution)/shard_map/output/pallas_call | solution.py:549
  61.0 1.0 %copy.17 = bf16[64,8192]{1,0:T(8,128)(2,1)} copy(bf16[64,8192]{1,0:T(8,128)(2,1)S(1)} %output.1) | data formatting | bytes 2097152
Async XLA Ops:
  0.6 13.0 %copy-start = (s32[64]{0:T(128)S(1)}, s32[64]{0:T(128)}, u32[]{:S(2)}) copy-start(s32[64]{0:T(128)} %pos.3) | copy-start | bytes 772

commit v4 on v3

--- a/solution.py
+++ b/solution.py
@@ -14,7 +14,7 @@
 F32 = jnp.float32
 BF16 = jnp.bfloat16
 TILES = 16
-FIRST = 6
+FIRST = 8
 MOST = max(FIRST, TILES - FIRST)
 HALVES = 2
 NS = 4

time: 62.1 us -> 61.4 us (0.989)
  Pallas kernels: 60.3 us -> 59.6 us
    pallas_call x1, Pallas kernels: 39.9 us -> 39.2 us  [local_step(): pl.pallas_call(output_kernel, out_shape=pltpu.VMEM((batch, d_model), BF16...]
where the time goes in v4:
time: 61.4 us; the launch traced here: 61.2 us
  Pallas kernels  59.6 us (97%)
  local copies, waits for them, and re-layouts  0.98 us (2%)
  between operations  0.67 us (1%)
    pallas_call x1, Pallas kernels, local_step(): pl.pallas_call(output_kernel, out_shape=pltpu.VMEM((batch, d_model), BF16...  39.2 us
    pallas_call x1, Pallas kernels, local_step(): pl.pallas_call(qkv_kernel, out_shape=(acc_type, pltpu.VMEM((2, 2, batch,...  13 us
    pallas_call x1, Pallas kernels, local_step(): pl.pallas_call(attention_kernel, out_shape=(jax.ShapeDtypeStruct(cache, B...  7.39 us

profile of v4, /device:TPU:0, one launch (start us, length us, event | category | flops | bytes accessed | tf_op | source)
XLA Modules:
  0.0 61.2 jit_solution(13362781980205554074)
XLA Ops:
  0.6 0.0 copy-start
  0.6 13.0 %qkv.1 = (f32[1024,128]{1,0:T(8,128)S(1)}, f32[2,2,64,128]{3,2,1,0:T(8,128)S(1)}, bf16[64,512,128]{2,1,0:T(8,128)(2,1)S(1)}, bf16[64,512,128]{2,1,0:T(8,128)(2,1)S(1)}) custom-call(s32[64]{0:T(128)} %pos.3, bf16[64,8192]{1,0:T(8,128)(2,1)} %hid.3, f32[1,8192]{1,0:T(1,128)} %bitcast.9, bf16[8192,2048]{1,0:T(8,128)(2,1)} %wq.1, bf16[8192,256]{1,0:T(8,128)(2,1)} %wk.1, ...), custom_call_target="tpu_custom_call" | custom-call | tf_op jit(solution)/shard_map/qkv/pallas_call | solution.py:497
  13.7 0.0 copy-done
  13.7 7.4 %attention.1 = (bf16[64,512,128]{2,1,0:T(8,128)(2,1)}, bf16[64,512,128]{2,1,0:T(8,128)(2,1)}, f32[1024,128]{1,0:T(8,128)S(1)}, f32[64,128]{1,0:T(8,128)S(1)}, bf...) custom-call(s32[64]{0:T(128)S(1)} %copy-done, ...), custom_call_target="tpu_custom_call", output_to_operand_aliasing={{4}: (3, {}), {5}: (4, {})} | custom-call | tf_op jit(solution)/shard_map/attention/pallas_call | solution.py:523
  21.1 39.2 %output.1 = bf16[64,8192]{1,0:T(8,128)(2,1)S(1)} custom-call(f32[16,64,128]{2,1,0:T(8,128)S(1)} %bitcast.6, f32[64,128]{1,0:T(8,128)S(1)} %get-tuple-element.16.stat, bf16[64,8192]{1,0:T(8,128)(2,1)} %hid.3, bf16[2048,8192]{1,0:T(8,128)(2,1)} %wo.1), custom_call_target="tpu_custom_call" | custom-call | tf_op jit(solution)/shard_map/output/pallas_call | solution.py:549
  60.3 1.0 %copy.17 = bf16[64,8192]{1,0:T(8,128)(2,1)} copy(bf16[64,8192]{1,0:T(8,128)(2,1)S(1)} %output.1) | data formatting | bytes 2097152
Async XLA Ops:
  0.6 13.0 %copy-start = (s32[64]{0:T(128)S(1)}, s32[64]{0:T(128)}, u32[]{:S(2)}) copy-start(s32[64]{0:T(128)} %pos.3) | copy-start | bytes 772

commit v5 on v4

--- a/solution.py
+++ b/solution.py
@@ -18,7 +18,7 @@
 MOST = max(FIRST, TILES - FIRST)
 HALVES = 2
 NS = 4
-LAG = 4
+LAG = 6
 
 
 def remote(src, dst, send, recv, device):

time: 61.4 us -> 60.5 us (0.985)
  Pallas kernels: 59.6 us -> 58.7 us
    pallas_call x1, Pallas kernels: 39.2 us -> 38.3 us  [local_step(): pl.pallas_call(output_kernel, out_shape=pltpu.VMEM((batch, d_model), BF16...]
where the time goes in v5:
time: 60.5 us; the launch traced here: 60.3 us
  Pallas kernels  58.7 us (97%)
  local copies, waits for them, and re-layouts  0.98 us (2%)
  between operations  0.67 us (1%)
    pallas_call x1, Pallas kernels, local_step(): pl.pallas_call(output_kernel, out_shape=pltpu.VMEM((batch, d_model), BF16...  38.3 us
    pallas_call x1, Pallas kernels, local_step(): pl.pallas_call(qkv_kernel, out_shape=(acc_type, pltpu.VMEM((2, 2, batch,...  13 us
    pallas_call x1, Pallas kernels, local_step(): pl.pallas_call(attention_kernel, out_shape=(jax.ShapeDtypeStruct(cache, B...  7.39 us

profile of v5, /device:TPU:0, one launch (start us, length us, event | category | flops | bytes accessed | tf_op | source)
XLA Modules:
  0.0 60.3 jit_solution(3137434209968540233)
XLA Ops:
  0.6 0.0 copy-start
  0.6 13.0 %qkv.1 = (f32[1024,128]{1,0:T(8,128)S(1)}, f32[2,2,64,128]{3,2,1,0:T(8,128)S(1)}, bf16[64,512,128]{2,1,0:T(8,128)(2,1)S(1)}, bf16[64,512,128]{2,1,0:T(8,128)(2,1)S(1)}) custom-call(s32[64]{0:T(128)} %pos.3, bf16[64,8192]{1,0:T(8,128)(2,1)} %hid.3, f32[1,8192]{1,0:T(1,128)} %bitcast.9, bf16[8192,2048]{1,0:T(8,128)(2,1)} %wq.1, bf16[8192,256]{1,0:T(8,128)(2,1)} %wk.1, ...), custom_call_target="tpu_custom_call" | custom-call | tf_op jit(solution)/shard_map/qkv/pallas_call | solution.py:497
  13.7 0.0 copy-done
  13.7 7.4 %attention.1 = (bf16[64,512,128]{2,1,0:T(8,128)(2,1)}, bf16[64,512,128]{2,1,0:T(8,128)(2,1)}, f32[1024,128]{1,0:T(8,128)S(1)}, f32[64,128]{1,0:T(8,128)S(1)}, bf...) custom-call(s32[64]{0:T(128)S(1)} %copy-done, ...), custom_call_target="tpu_custom_call", output_to_operand_aliasing={{4}: (3, {}), {5}: (4, {})} | custom-call | tf_op jit(solution)/shard_map/attention/pallas_call | solution.py:523
  21.1 38.3 %output.1 = bf16[64,8192]{1,0:T(8,128)(2,1)S(1)} custom-call(f32[16,64,128]{2,1,0:T(8,128)S(1)} %bitcast.6, f32[64,128]{1,0:T(8,128)S(1)} %get-tuple-element.16.stat, bf16[64,8192]{1,0:T(8,128)(2,1)} %hid.3, bf16[2048,8192]{1,0:T(8,128)(2,1)} %wo.1), custom_call_target="tpu_custom_call" | custom-call | tf_op jit(solution)/shard_map/output/pallas_call | solution.py:549
  59.3 1.0 %copy.17 = bf16[64,8192]{1,0:T(8,128)(2,1)} copy(bf16[64,8192]{1,0:T(8,128)(2,1)S(1)} %output.1) | data formatting | bytes 2097152
Async XLA Ops:
  0.6 13.0 %copy-start = (s32[64]{0:T(128)S(1)}, s32[64]{0:T(128)}, u32[]{:S(2)}) copy-start(s32[64]{0:T(128)} %pos.3) | copy-start | bytes 772

commit v6 on v5

--- a/solution.py
+++ b/solution.py
@@ -13,12 +13,13 @@
 MESH = pl.DeviceIdType.MESH
 F32 = jnp.float32
 BF16 = jnp.bfloat16
-TILES = 16
-FIRST = 8
-MOST = max(FIRST, TILES - FIRST)
+TILES = 8
 HALVES = 2
+COUNT = TILES * HALVES
 NS = 4
-LAG = 6
+LAG_Z = 5
+LAG_Y = 5
+GROUP = 4
 
 
 def remote(src, dst, send, recv, device):
@@ -103,11 +104,10 @@
     def rotate(x):
         return x * cosf + pltpu.roll(x, 64, 1) * sinf
 
-    def span(p):
-        return pl.ds(4, 1) if p == 0 else pl.ds(2 * (p - 1), 2)
+    order = (4, 0, 1, 2, 3)
 
     def exchange(kind, owner, p, device):
-        part = pieces.at[owner, span(p)]
+        part = pieces.at[owner, p]
         return remote(part, part, xsem.at[2 * kind, p], xsem.at[2 * kind + 1, p], device)
 
     def publish(p):
@@ -118,7 +118,7 @@
     kv = jnp.dot(rbuf[...], wkvb[...], preferred_element_type=F32)
     pieces[me, 4] = round_bf16(jnp.where(keys, rotate(kv), kv))
     pl.semaphore_wait(barrier, 2)
-    publish(0)
+    publish(4)
     for t in range(tiles):
         wcopy(t).wait()
         if t == tiles - 1:
@@ -128,18 +128,18 @@
         q = jnp.dot(rbuf[...], wqb[t], preferred_element_type=F32)
         for h in range(2):
             pieces[me, 2 * t + h] = round_bf16(rotate(q[:, h * 128:(h + 1) * 128]))
-        publish(t + 1)
-    for p in range(tiles + 1):
+            publish(2 * t + h)
+    for p in order:
         exchange(0, me, p, ynbr).wait_recv()
         exchange(2, across, p, partner).start()
-    for p in range(tiles + 1):
+    for p in order:
         exchange(1, me, p, partner).wait_recv()
         exchange(2, across, p, partner).wait_recv()
     for owner in range(4):
         for h in range(4):
             q_out[pl.ds((owner * 4 + h) * batch, batch), :] = pieces[owner, h]
         kv_out[owner % 2, owner // 2] = pieces[owner, 4]
-    for p in range(tiles + 1):
+    for p in order:
         exchange(0, me, p, ynbr).wait_send()
         exchange(1, me, p, partner).wait_send()
         exchange(2, across, p, partner).wait_send()
@@ -218,7 +218,7 @@
 def output_kernel(
     acc, stat, hid, wo, out,
     hbuf, wob, obf, acc_p, acc_c, acc_y, o_own, o_land, st_p, st_c, st_y, part, land_a, land_b, tot,
-    lsem, stsem, dsem, fsem,
+    lsem, stsem, dsem, fsem, rsem, esem,
 ):
     z = lax.axis_index("tp")
     me = lax.axis_index("sp")
@@ -237,14 +237,11 @@
     tile = wob.shape[2]
     rows_s = batch // NS
     rows_h = batch // HALVES
-    mine_n = jnp.where(core == 0, FIRST, TILES - FIRST)
-    mate_n = TILES - mine_n
-
-    hcopy = pltpu.make_async_copy(hid, hbuf, lsem.at[MOST])
+
+    hcopy = pltpu.make_async_copy(hid, hbuf, lsem.at[TILES])
 
     def columns(quarter, t):
-        first = (quarter // 2) * TILES + lax.rem(quarter, 2) * FIRST
-        return pl.ds(pl.multiple_of((first + t) * tile, tile), tile)
+        return pl.ds(pl.multiple_of((quarter * TILES + t) * tile, tile), tile)
 
     def wcopy(t):
         return pltpu.make_async_copy(wo.at[:, columns(me, t)], wob.at[t], lsem.at[t])
@@ -268,7 +265,7 @@
     def _():
         pl.semaphore_signal(barrier, inc=1, device_id={"tp": z + 1}, device_id_type=MESH)
 
-    repeat(0, mine_n, lambda t: wcopy(t).start())
+    repeat(0, TILES, lambda t: wcopy(t).start())
     hcopy.start()
 
     @pl.when(outer)
@@ -325,22 +322,38 @@
     o_send = []
 
     def send_a(j):
-        return remote(part.at[j], land_a.at[j], fsem.at[0, j], fsem.at[1, j], {"tp": z_in})
+        return remote(part.at[j], land_a.at[j], fsem.at[0], rsem.at[0, j], {"tp": z_in})
 
     def send_b(j):
-        return remote(part.at[j], land_b.at[j], fsem.at[2, j], fsem.at[3, j], {"tp": z_in})
+        return remote(part.at[j], land_b.at[j], fsem.at[1], rsem.at[1, j], {"tp": z_in})
 
     def send_c(j):
-        return remote(tot.at[me, j], tot.at[me, j], fsem.at[4, j], fsem.at[5, j], {"tp": z_out})
+        return remote(tot.at[me, j], tot.at[me, j], fsem.at[2], rsem.at[2, j], {"tp": z_out})
 
     def send_d(j):
-        return remote(tot.at[me, j], tot.at[me, j], fsem.at[6, j], fsem.at[7, j], ynbr)
+        return remote(tot.at[me, j], tot.at[me, j], fsem.at[3], rsem.at[3, j], ynbr)
 
     def send_e(j):
-        return remote(tot.at[me, j], tot.at[me, j], fsem.at[8, j], fsem.at[9, j], partner)
+        return remote(tot.at[me, j], tot.at[me, j], fsem.at[4], esem.at[0, j // GROUP], partner)
 
     def send_f(j):
-        return remote(tot.at[across, j], tot.at[across, j], fsem.at[10, j], fsem.at[11, j], partner)
+        return remote(tot.at[across, j], tot.at[across, j], fsem.at[5], esem.at[1, j // GROUP], partner)
+
+    def project(half, t):
+        if half == 0:
+            wcopy(t).wait()
+        j = half * TILES + t
+        part[j] = jnp.dot(obf[half * rows_h:(half + 1) * rows_h, :], wob[t], preferred_element_type=F32)
+
+    def project_send(half):
+        def step(t):
+            project(half, t)
+
+            @pl.when(outer)
+            def _():
+                send_a(half * TILES + t).start()
+
+        repeat(0, TILES, step)
 
     for half in range(HALVES):
         chunks = range(half * NS // HALVES, (half + 1) * NS // HALVES)
@@ -361,111 +374,97 @@
             for h in range(mine):
                 obf[sl, pl.ds(pl.multiple_of(((1 - core) * mine + h) * hd, hd), hd)] = o_land[h, sl, :].astype(BF16)
 
-        def project(t, half=half):
-            if half == 0:
-                wcopy(t).wait()
-            j = half * mine_n + t
-            part[j] = jnp.dot(obf[half * rows_h:(half + 1) * rows_h, :], wob[t], preferred_element_type=F32)
-
-            @pl.when(outer)
-            def _():
-                send_a(j).start()
-
-        repeat(0, mine_n, project)
+        if half < HALVES - 1:
+            project_send(half)
     hcopy.wait()
 
-    def emit(quarter, count, j):
-        half = j // count
+    def emit(quarter, j):
+        half = j // TILES
         rows = pl.ds(pl.multiple_of(half * rows_h, rows_h), rows_h)
-        where = columns(quarter, j - half * count)
+        where = columns(quarter, j - half * TILES)
         out[rows, where] = (hbuf[rows, where].astype(F32) + tot[quarter, j]).astype(BF16)
 
     def share(j):
         send_d(j).start()
         send_e(j).start()
-        emit(me, mine_n, j)
-
-    def collect_y(j):
-        send_d(j).wait_recv()
-        send_f(j).start()
-        emit(across, mine_n, j)
-
-    def collect_core(j):
-        send_e(j).wait_recv()
-        emit(mate, mate_n, j)
-
-    def last(j):
-        send_f(j).wait_recv()
-        emit(diagonal, mate_n, j)
-
-    mine_c = HALVES * mine_n
-    mate_c = HALVES * mate_n
-
-    def collect(k):
-        @pl.when(k >= 0)
+        emit(me, j)
+
+    def collect(j):
+        @pl.when(j >= 0)
         def _():
-            collect_y(k)
-
-        @pl.when(jnp.logical_and(k >= 0, k < mate_c))
-        def _():
-            collect_core(k)
+            send_d(j).wait_recv()
+            send_f(j).start()
+            emit(across, j)
+
+    def gather(kind, owner, g):
+        group = tot.at[owner, pl.ds(g * GROUP, GROUP)]
+        remote(group, group, fsem.at[4 + kind], esem.at[kind, g], partner).wait_recv()
+        repeat(g * GROUP, (g + 1) * GROUP, lambda j: emit(owner, j))
+
+    groups = COUNT // GROUP
+
+    def trickle(j, last):
+        for g in range(groups):
+            @pl.when(j == last - groups + g)
+            def _(g=g):
+                gather(0, mate, g)
 
     @pl.when(outer)
     def _():
+        project_send(HALVES - 1)
+
         def step(j):
-            @pl.when(j < mine_c)
+            @pl.when(j < COUNT)
             def _():
                 send_c(j).wait_recv()
                 share(j)
 
-            collect(j - LAG)
-
-        repeat(0, mine_c + LAG, step)
-        repeat(0, mine_c, lambda j: send_a(j).wait_send())
+            collect(j - LAG_Y)
+            trickle(j, COUNT + LAG_Y)
+
+        repeat(0, COUNT + LAG_Y, step)
+        remote(part, land_a, fsem.at[0], rsem.at[0, 0], {"tp": z_in}).wait_send()
 
     @pl.when(inner)
     def _():
         def step(j):
-            @pl.when(j < mine_c)
+            @pl.when(j < TILES)
+            def _():
+                project(HALVES - 1, j)
+
+            @pl.when(j < COUNT)
             def _():
                 send_a(j).wait_recv()
                 part[j] = part[j] + land_a[j]
                 send_b(j).start()
 
-            k = j - LAG
-
-            @pl.when(jnp.logical_and(k >= 0, k < mine_c))
+            k = j - LAG_Z
+
+            @pl.when(jnp.logical_and(k >= 0, k < COUNT))
             def _():
                 send_b(k).wait_recv()
                 tot[me, k] = part[k] + land_b[k]
                 send_c(k).start()
                 share(k)
 
-            collect(j - 2 * LAG)
-
-        repeat(0, mine_c + 2 * LAG, step)
-
-        def drain(j):
-            send_b(j).wait_send()
-            send_c(j).wait_send()
-
-        repeat(0, mine_c, drain)
-
-    repeat(mine_c, mate_c, collect_core)
-    repeat(0, mate_c, last)
+            collect(k - LAG_Y)
+            trickle(j, COUNT + LAG_Z + LAG_Y)
+
+        repeat(0, COUNT + LAG_Z + LAG_Y, step)
+        remote(part, land_b, fsem.at[1], rsem.at[1, 0], {"tp": z_in}).wait_send()
+        remote(tot.at[me], tot.at[me], fsem.at[2], rsem.at[2, 0], {"tp": z_out}).wait_send()
+
+    for g in range(groups):
+        gather(1, diagonal, g)
     st_send.wait_send()
     sty_send.wait_send()
     for s in range(NS):
         p_send[s].wait_send()
         y_send[s].wait_send()
         o_send[s].wait_send()
-
-    def finish(j):
-        send_d(j).wait_send()
-        send_e(j).wait_send()
-        send_f(j).wait_send()
-
-    repeat(0, mine_c, finish)
+    remote(tot.at[me], tot.at[me], fsem.at[3], rsem.at[3, 0], ynbr).wait_send()
+    remote(tot.at[me], tot.at[me], fsem.at[4], esem.at[0, 0], partner).wait_send()
+    remote(tot.at[across], tot.at[across], fsem.at[5], esem.at[1, 0], partner).wait_send()
 
 
 def solution(mesh):
@@ -511,7 +510,7 @@
                 dma((3,)),
                 dma((tiles,)),
                 dma((2, 4)),
-                dma((6, tiles + 1)),
+                dma((6, 5)),
             ],
             compiler_params=params(24, 0),
             name="qkv",
@@ -540,12 +539,11 @@
         )(positions, keep(q), keep(kv), keep(k_in), keep(v_in))
 
         mine = heads // 2
-        ocols = d_model // 2 // TILES
+        ocols = d_model // 4 // TILES
         buf = pltpu.VMEM((mine, batch, hd), F32)
         st = pltpu.VMEM((batch, hd), F32)
-        messages = HALVES * MOST
         block = (batch // HALVES, ocols)
-        chunk = pltpu.VMEM((messages,) + block, F32)
+        chunk = pltpu.VMEM((COUNT,) + block, F32)
         out = pl.pallas_call(
             output_kernel,
             out_shape=pltpu.VMEM((batch, d_model), BF16),
@@ -553,14 +551,16 @@
             out_specs=vmem,
             scratch_shapes=[
                 pltpu.VMEM((batch, d_model), BF16),
-                pltpu.VMEM((MOST, q_cols, ocols), BF16),
+                pltpu.VMEM((TILES, q_cols, ocols), BF16),
                 pltpu.VMEM((batch, q_cols), BF16),
                 buf, buf, buf, buf, buf, st, st, st, chunk, chunk, chunk,
-                pltpu.VMEM((4, messages) + block, F32),
-                dma((MOST + 1,)),
+                pltpu.VMEM((4, COUNT) + block, F32),
+                dma((TILES + 1,)),
                 dma((4,)),
                 dma((6, NS)),
-                dma((12, messages)),
+                dma((6,)),
+                dma((4, COUNT)),
+                dma((2, COUNT // GROUP)),
             ],
             compiler_params=params(28, 1),
             name="output",

time: 60.5 us -> 57.9 us (0.957)
  Pallas kernels: 58.7 us -> 56.1 us
    pallas_call x1, Pallas kernels: 38.3 us -> 35.6 us  [local_step(): pl.pallas_call(output_kernel, out_shape=pltpu.VMEM((batch, d_model), BF16...]
where the time goes in v6:
time: 57.9 us; the launch traced here: 57.7 us
  Pallas kernels  56.1 us (97%)
  local copies, waits for them, and re-layouts  0.98 us (2%)
  between operations  0.67 us (1%)
    pallas_call x1, Pallas kernels, local_step(): pl.pallas_call(output_kernel, out_shape=pltpu.VMEM((batch, d_model), BF16...  35.6 us
    pallas_call x1, Pallas kernels, local_step(): pl.pallas_call(qkv_kernel, out_shape=(acc_type, pltpu.VMEM((2, 2, batch,...  13.1 us
    pallas_call x1, Pallas kernels, local_step(): pl.pallas_call(attention_kernel, out_shape=(jax.ShapeDtypeStruct(cache, B...  7.39 us

profile of v6, /device:TPU:0, one launch (start us, length us, event | category | flops | bytes accessed | tf_op | source)
XLA Modules:
  0.0 57.7 jit_solution(5662349859627686688)
XLA Ops:
  0.6 0.0 copy-start
  0.6 13.1 %qkv.1 = (f32[1024,128]{1,0:T(8,128)S(1)}, f32[2,2,64,128]{3,2,1,0:T(8,128)S(1)}, bf16[64,512,128]{2,1,0:T(8,128)(2,1)S(1)}, bf16[64,512,128]{2,1,0:T(8,128)(2,1)S(1)}) custom-call(s32[64]{0:T(128)} %pos.3, bf16[64,8192]{1,0:T(8,128)(2,1)} %hid.3, f32[1,8192]{1,0:T(1,128)} %bitcast.9, bf16[8192,2048]{1,0:T(8,128)(2,1)} %wq.1, bf16[8192,256]{1,0:T(8,128)(2,1)} %wk.1, ...), custom_call_target="tpu_custom_call" | custom-call | tf_op jit(solution)/shard_map/qkv/pallas_call | solution.py:496
  13.7 0.0 copy-done
  13.7 7.4 %attention.1 = (bf16[64,512,128]{2,1,0:T(8,128)(2,1)}, bf16[64,512,128]{2,1,0:T(8,128)(2,1)}, f32[1024,128]{1,0:T(8,128)S(1)}, f32[64,128]{1,0:T(8,128)S(1)}, bf...) custom-call(s32[64]{0:T(128)S(1)} %copy-done, ...), custom_call_target="tpu_custom_call", output_to_operand_aliasing={{4}: (3, {}), {5}: (4, {})} | custom-call | tf_op jit(solution)/shard_map/attention/pallas_call | solution.py:522
  21.1 35.6 %output.1 = bf16[64,8192]{1,0:T(8,128)(2,1)S(1)} custom-call(f32[16,64,128]{2,1,0:T(8,128)S(1)} %bitcast.6, f32[64,128]{1,0:T(8,128)S(1)} %get-tuple-element.16.stat, bf16[64,8192]{1,0:T(8,128)(2,1)} %hid.3, bf16[2048,8192]{1,0:T(8,128)(2,1)} %wo.1), custom_call_target="tpu_custom_call" | custom-call | tf_op jit(solution)/shard_map/output/pallas_call | solution.py:547
  56.7 1.0 %copy.17 = bf16[64,8192]{1,0:T(8,128)(2,1)} copy(bf16[64,8192]{1,0:T(8,128)(2,1)S(1)} %output.1) | data formatting | bytes 2097152
Async XLA Ops:
  0.6 13.1 %copy-start = (s32[64]{0:T(128)S(1)}, s32[64]{0:T(128)}, u32[]{:S(2)}) copy-start(s32[64]{0:T(128)} %pos.3) | copy-start | bytes 772

commit v7 on v6

--- a/solution.py
+++ b/solution.py
@@ -13,10 +13,10 @@
 MESH = pl.DeviceIdType.MESH
 F32 = jnp.float32
 BF16 = jnp.bfloat16
-TILES = 8
-HALVES = 2
-COUNT = TILES * HALVES
-NS = 4
+TILES = 4
+BLOCKS = 4
+COUNT = TILES * BLOCKS
+DIRECT = 2
 LAG_Z = 5
 LAG_Y = 5
 GROUP = 4
@@ -235,8 +235,7 @@
     heads, batch, hd = acc.shape
     mine = heads // 2
     tile = wob.shape[2]
-    rows_s = batch // NS
-    rows_h = batch // HALVES
+    rows_b = batch // BLOCKS
 
     hcopy = pltpu.make_async_copy(hid, hbuf, lsem.at[TILES])
 
@@ -270,19 +269,21 @@
 
     @pl.when(outer)
     def _():
-        pl.semaphore_wait(barrier, 3)
+        pl.semaphore_signal(barrier, inc=1, device_id={"sp": across, "tp": z_in}, device_id_type=MESH)
+        pl.semaphore_wait(barrier, 4)
 
     @pl.when(inner)
     def _():
-        pl.semaphore_wait(barrier, 4)
+        pl.semaphore_signal(barrier, inc=1, device_id={"sp": across, "tp": z_out}, device_id_type=MESH)
+        pl.semaphore_wait(barrier, 5)
 
     def part_rows(s):
-        return pl.ds(s * rows_s, rows_s)
+        return pl.ds(s * rows_b, rows_b)
 
     st_send = remote(stat, st_p, stsem.at[0], stsem.at[1], partner)
     st_send.start()
     p_send = []
-    for s in range(NS):
+    for s in range(BLOCKS):
         copy = remote(
             acc.at[pl.ds((1 - core) * mine, mine), part_rows(s)], acc_p.at[:, part_rows(s)],
             dsem.at[0, s], dsem.at[1, s], partner,
@@ -306,19 +307,19 @@
     st_send.wait_recv()
     top, ea, eb, total = merge(own_heads(stat[...]), own_heads(st_p[...]))
     st_c[...] = jnp.where(lane < heads, top, pltpu.roll(total, heads, 1))
-    sty_send = remote(st_c, st_y, stsem.at[2], stsem.at[3], ynbr)
-    sty_send.start()
     y_send = []
-    for s in range(NS):
+    sty_send = []
+    for s in range(BLOCKS):
         p_send[s].wait_recv()
-        sl = slice(s * rows_s, (s + 1) * rows_s)
+        sl = slice(s * rows_b, (s + 1) * rows_b)
         for h in range(mine):
             acc_c[h, sl, :] = acc[core * mine + h, sl, :] * ea[sl, h:h + 1] + acc_p[h, sl, :] * eb[sl, h:h + 1]
+        copy = remote(st_c.at[part_rows(s)], st_y.at[part_rows(s)], stsem.at[2], stsem.at[3 + s], ynbr)
+        copy.start()
+        sty_send.append(copy)
         copy = remote(acc_c.at[:, part_rows(s)], acc_y.at[:, part_rows(s)], dsem.at[2, s], dsem.at[3, s], ynbr)
         copy.start()
         y_send.append(copy)
-    sty_send.wait_recv()
-    _, ea, eb, total = merge(st_c[...], st_y[...])
     o_send = []
 
     def send_a(j):
@@ -339,53 +340,55 @@
     def send_f(j):
         return remote(tot.at[across, j], tot.at[across, j], fsem.at[5], esem.at[1, j // GROUP], partner)
 
-    def project(half, t):
-        if half == 0:
-            wcopy(t).wait()
-        j = half * TILES + t
-        part[j] = jnp.dot(obf[half * rows_h:(half + 1) * rows_h, :], wob[t], preferred_element_type=F32)
-
-    def project_send(half):
-        def step(t):
-            project(half, t)
-
+    def project(j):
+        rows = pl.ds(pl.multiple_of((j // TILES) * rows_b, rows_b), rows_b)
+        part[j] = jnp.dot(obf[rows, :], wob[lax.rem(j, TILES)], preferred_element_type=F32)
+
+    for s in range(BLOCKS):
+        sl = slice(s * rows_b, (s + 1) * rows_b)
+        sty_send[s].wait_recv()
+        _, ea, eb, total = merge(st_c[sl, :], st_y[sl, :])
+        y_send[s].wait_recv()
+        for h in range(mine):
+            o = acc_c[h, sl, :] * ea[:, h:h + 1] + acc_y[h, sl, :] * eb[:, h:h + 1]
+            o = round_bf16(o / total[:, h:h + 1])
+            o_own[h, sl, :] = o
+            obf[sl, pl.ds(pl.multiple_of((core * mine + h) * hd, hd), hd)] = o.astype(BF16)
+        copy = remote(o_own.at[:, part_rows(s)], o_land.at[:, part_rows(s)], dsem.at[4, s], dsem.at[5, s], partner)
+        copy.start()
+        o_send.append(copy)
+        copy.wait_recv()
+        for h in range(mine):
+            obf[sl, pl.ds(pl.multiple_of(((1 - core) * mine + h) * hd, hd), hd)] = o_land[h, sl, :].astype(BF16)
+        if s == 0:
+            def first_block(t):
+                wcopy(t).wait()
+                project(t)
+
+                @pl.when(outer)
+                def _():
+                    send_a(t).start()
+
+            repeat(0, TILES, first_block)
+        else:
             @pl.when(outer)
-            def _():
-                send_a(half * TILES + t).start()
-
-        repeat(0, TILES, step)
-
-    for half in range(HALVES):
-        chunks = range(half * NS // HALVES, (half + 1) * NS // HALVES)
-        for s in chunks:
-            y_send[s].wait_recv()
-            sl = slice(s * rows_s, (s + 1) * rows_s)
-            for h in range(mine):
-                o = acc_c[h, sl, :] * ea[sl, h:h + 1] + acc_y[h, sl, :] * eb[sl, h:h + 1]
-                o = round_bf16(o / total[sl, h:h + 1])
-                o_own[h, sl, :] = o
-                obf[sl, pl.ds(pl.multiple_of((core * mine + h) * hd, hd), hd)] = o.astype(BF16)
-            copy = remote(o_own.at[:, part_rows(s)], o_land.at[:, part_rows(s)], dsem.at[4, s], dsem.at[5, s], partner)
-            copy.start()
-            o_send.append(copy)
-        for s in chunks:
-            o_send[s].wait_recv()
-            sl = slice(s * rows_s, (s + 1) * rows_s)
-            for h in range(mine):
-                obf[sl, pl.ds(pl.multiple_of(((1 - core) * mine + h) * hd, hd), hd)] = o_land[h, sl, :].astype(BF16)
-
-        if half < HALVES - 1:
-            project_send(half)
+            def _(s=s):
+                def next_block(j):
+                    project(j)
+                    send_a(j).start()
+
+                repeat(s * TILES, (s + 1) * TILES, next_block)
     hcopy.wait()
 
     def emit(quarter, j):
-        half = j // TILES
-        rows = pl.ds(pl.multiple_of(half * rows_h, rows_h), rows_h)
-        where = columns(quarter, j - half * TILES)
+        rows = pl.ds(pl.multiple_of((j // TILES) * rows_b, rows_b), rows_b)
+        where = columns(quarter, lax.rem(j, TILES))
         out[rows, where] = (hbuf[rows, where].astype(F32) + tot[quarter, j]).astype(BF16)
 
+    def send_x(j):
+        return remote(tot.at[me, j], tot.at[me, j], fsem.at[6], rsem.at[3, j], {"sp": across, "tp": z_out})
+
     def share(j):
-        send_d(j).start()
         send_e(j).start()
         emit(me, j)
 
@@ -411,12 +414,15 @@
 
     @pl.when(outer)
     def _():
-        project_send(HALVES - 1)
-
         def step(j):
             @pl.when(j < COUNT)
             def _():
                 send_c(j).wait_recv()
+
+                @pl.when(j < COUNT - DIRECT)
+                def _():
+                    send_d(j).start()
+
                 share(j)
 
             collect(j - LAG_Y)
@@ -424,13 +430,15 @@
 
         repeat(0, COUNT + LAG_Y, step)
         remote(part, land_a, fsem.at[0], rsem.at[0, 0], {"tp": z_in}).wait_send()
+        sent = tot.at[me, pl.ds(0, COUNT - DIRECT)]
+        remote(sent, sent, fsem.at[3], rsem.at[3, 0], ynbr).wait_send()
 
     @pl.when(inner)
     def _():
         def step(j):
-            @pl.when(j < TILES)
+            @pl.when(j < COUNT - TILES)
             def _():
-                project(HALVES - 1, j)
+                project(TILES + j)
 
             @pl.when(j < COUNT)
             def _():
@@ -445,6 +453,12 @@
                 send_b(k).wait_recv()
                 tot[me, k] = part[k] + land_b[k]
                 send_c(k).start()
+                send_d(k).start()
+
+                @pl.when(k >= COUNT - DIRECT)
+                def _():
+                    send_x(k).start()
+
                 share(k)
 
             collect(k - LAG_Y)
@@ -453,16 +467,18 @@
         repeat(0, COUNT + LAG_Z + LAG_Y, step)
         remote(part, land_b, fsem.at[1], rsem.at[1, 0], {"tp": z_in}).wait_send()
         remote(tot.at[me], tot.at[me], fsem.at[2], rsem.at[2, 0], {"tp": z_out}).wait_send()
+        remote(tot.at[me], tot.at[me], fsem.at[3], rsem.at[3, 0], ynbr).wait_send()
+        sent = tot.at[me, pl.ds(0, DIRECT)]
+        remote(sent, sent, fsem.at[6], rsem.at[3, 0], ynbr).wait_send()
 
     for g in range(groups):
         gather(1, diagonal, g)
     st_send.wait_send()
-    sty_send.wait_send()
-    for s in range(NS):
+    remote(st_c, st_y, stsem.at[2], stsem.at[3], ynbr).wait_send()
+    for s in range(BLOCKS):
         p_send[s].wait_send()
         y_send[s].wait_send()
         o_send[s].wait_send()
-    remote(tot.at[me], tot.at[me], fsem.at[3], rsem.at[3, 0], ynbr).wait_send()
     remote(tot.at[me], tot.at[me], fsem.at[4], esem.at[0, 0], partner).wait_send()
     remote(tot.at[across], tot.at[across], fsem.at[5], esem.at[1, 0], partner).wait_send()
 
@@ -542,7 +558,7 @@
         ocols = d_model // 4 // TILES
         buf = pltpu.VMEM((mine, batch, hd), F32)
         st = pltpu.VMEM((batch, hd), F32)
-        block = (batch // HALVES, ocols)
+        block = (batch // BLOCKS, ocols)
         chunk = pltpu.VMEM((COUNT,) + block, F32)
         out = pl.pallas_call(
             output_kernel,
@@ -556,9 +572,9 @@
                 buf, buf, buf, buf, buf, st, st, st, chunk, chunk, chunk,
                 pltpu.VMEM((4, COUNT) + block, F32),
                 dma((TILES + 1,)),
-                dma((4,)),
-                dma((6, NS)),
-                dma((6,)),
+                dma((3 + BLOCKS,)),
+                dma((6, BLOCKS)),
+                dma((7,)),
                 dma((4, COUNT)),
                 dma((2, COUNT // GROUP)),
             ],

time: 57.9 us -> 58.7 us (1.014)
  Pallas kernels: 56.1 us -> 56.9 us
    pallas_call x1, Pallas kernels: 35.6 us -> 36.4 us  [local_step(): pl.pallas_call(output_kernel, out_shape=pltpu.VMEM((batch, d_model), BF16...]
where the time goes in v7:
time: 58.7 us; the launch traced here: 58.6 us
  Pallas kernels  56.9 us (97%)
  local copies, waits for them, and re-layouts  0.98 us (2%)
  between operations  0.67 us (1%)
    pallas_call x1, Pallas kernels, local_step(): pl.pallas_call(output_kernel, out_shape=pltpu.VMEM((batch, d_model), BF16...  36.4 us
    pallas_call x1, Pallas kernels, local_step(): pl.pallas_call(qkv_kernel, out_shape=(acc_type, pltpu.VMEM((2, 2, batch,...  13.1 us
    pallas_call x1, Pallas kernels, local_step(): pl.pallas_call(attention_kernel, out_shape=(jax.ShapeDtypeStruct(cache, B...  7.39 us

profile of v7, /device:TPU:0, one launch (start us, length us, event | category | flops | bytes accessed | tf_op | source)
XLA Modules:
  0.0 58.6 jit_solution(7842498642648252083)
XLA Ops:
  0.6 0.0 copy-start
  0.6 13.1 %qkv.1 = (f32[1024,128]{1,0:T(8,128)S(1)}, f32[2,2,64,128]{3,2,1,0:T(8,128)S(1)}, bf16[64,512,128]{2,1,0:T(8,128)(2,1)S(1)}, bf16[64,512,128]{2,1,0:T(8,128)(2,1)S(1)}) custom-call(s32[64]{0:T(128)} %pos.3, bf16[64,8192]{1,0:T(8,128)(2,1)} %hid.3, f32[1,8192]{1,0:T(1,128)} %bitcast.9, bf16[8192,2048]{1,0:T(8,128)(2,1)} %wq.1, bf16[8192,256]{1,0:T(8,128)(2,1)} %wk.1, ...), custom_call_target="tpu_custom_call" | custom-call | tf_op jit(solution)/shard_map/qkv/pallas_call | solution.py:512
  13.7 0.0 copy-done
  13.7 7.4 %attention.1 = (bf16[64,512,128]{2,1,0:T(8,128)(2,1)}, bf16[64,512,128]{2,1,0:T(8,128)(2,1)}, f32[1024,128]{1,0:T(8,128)S(1)}, f32[64,128]{1,0:T(8,128)S(1)}, bf...) custom-call(s32[64]{0:T(128)S(1)} %copy-done, ...), custom_call_target="tpu_custom_call", output_to_operand_aliasing={{4}: (3, {}), {5}: (4, {})} | custom-call | tf_op jit(solution)/shard_map/attention/pallas_call | solution.py:538
  21.1 36.4 %output.1 = bf16[64,8192]{1,0:T(8,128)(2,1)S(1)} custom-call(f32[16,64,128]{2,1,0:T(8,128)S(1)} %bitcast.6, f32[64,128]{1,0:T(8,128)S(1)} %get-tuple-element.16.stat, bf16[64,8192]{1,0:T(8,128)(2,1)} %hid.3, bf16[2048,8192]{1,0:T(8,128)(2,1)} %wo.1), custom_call_target="tpu_custom_call" | custom-call | tf_op jit(solution)/shard_map/output/pallas_call | solution.py:563
  57.6 1.0 %copy.17 = bf16[64,8192]{1,0:T(8,128)(2,1)} copy(bf16[64,8192]{1,0:T(8,128)(2,1)S(1)} %output.1) | data formatting | bytes 2097152
Async XLA Ops:
  0.6 13.1 %copy-start = (s32[64]{0:T(128)S(1)}, s32[64]{0:T(128)}, u32[]{:S(2)}) copy-start(s32[64]{0:T(128)} %pos.3) | copy-start | bytes 772

commit v8 on v7

--- a/solution.py
+++ b/solution.py
@@ -344,7 +344,7 @@
         rows = pl.ds(pl.multiple_of((j // TILES) * rows_b, rows_b), rows_b)
         part[j] = jnp.dot(obf[rows, :], wob[lax.rem(j, TILES)], preferred_element_type=F32)
 
-    for s in range(BLOCKS):
+    def values_send(s):
         sl = slice(s * rows_b, (s + 1) * rows_b)
         sty_send[s].wait_recv()
         _, ea, eb, total = merge(st_c[sl, :], st_y[sl, :])
@@ -357,27 +357,44 @@
         copy = remote(o_own.at[:, part_rows(s)], o_land.at[:, part_rows(s)], dsem.at[4, s], dsem.at[5, s], partner)
         copy.start()
         o_send.append(copy)
-        copy.wait_recv()
+
+    def values_recv(s):
+        sl = slice(s * rows_b, (s + 1) * rows_b)
+        o_send[s].wait_recv()
         for h in range(mine):
             obf[sl, pl.ds(pl.multiple_of(((1 - core) * mine + h) * hd, hd), hd)] = o_land[h, sl, :].astype(BF16)
-        if s == 0:
-            def first_block(t):
-                wcopy(t).wait()
-                project(t)
-
-                @pl.when(outer)
-                def _():
-                    send_a(t).start()
-
-            repeat(0, TILES, first_block)
-        else:
+
+    def first_tiles(low, high):
+        def tile_step(t):
+            wcopy(t).wait()
+            project(t)
+
             @pl.when(outer)
-            def _(s=s):
-                def next_block(j):
-                    project(j)
-                    send_a(j).start()
-
-                repeat(s * TILES, (s + 1) * TILES, next_block)
+            def _():
+                send_a(t).start()
+
+        repeat(low, high, tile_step)
+
+    def outer_tiles(low, high):
+        @pl.when(outer)
+        def _():
+            def tile_step(j):
+                project(j)
+                send_a(j).start()
+
+            repeat(low, high, tile_step)
+
+    values_send(0)
+    values_recv(0)
+    for s in range(BLOCKS):
+        tiles_of = first_tiles if s == 0 else outer_tiles
+        middle = s * TILES + TILES // 2
+        tiles_of(s * TILES, middle)
+        if s < BLOCKS - 1:
+            values_send(s + 1)
+        tiles_of(middle, (s + 1) * TILES)
+        if s < BLOCKS - 1:
+            values_recv(s + 1)
     hcopy.wait()
 
     def emit(quarter, j):

time: 58.7 us -> 58 us (0.988)
  Pallas kernels: 56.9 us -> 56.2 us
    pallas_call x1, Pallas kernels: 36.4 us -> 35.8 us  [local_step(): pl.pallas_call(output_kernel, out_shape=pltpu.VMEM((batch, d_model), BF16...]
where the time goes in v8:
time: 58 us; the launch traced here: 57.9 us
  Pallas kernels  56.2 us (97%)
  local copies, waits for them, and re-layouts  0.98 us (2%)
  between operations  0.67 us (1%)
    pallas_call x1, Pallas kernels, local_step(): pl.pallas_call(output_kernel, out_shape=pltpu.VMEM((batch, d_model), BF16...  35.8 us
    pallas_call x1, Pallas kernels, local_step(): pl.pallas_call(qkv_kernel, out_shape=(acc_type, pltpu.VMEM((2, 2, batch,...  13.1 us
    pallas_call x1, Pallas kernels, local_step(): pl.pallas_call(attention_kernel, out_shape=(jax.ShapeDtypeStruct(cache, B...  7.39 us

profile of v8, /device:TPU:0, one launch (start us, length us, event | category | flops | bytes accessed | tf_op | source)
XLA Modules:
  0.0 57.9 jit_solution(3794863155060112495)
XLA Ops:
  0.6 0.0 copy-start
  0.6 13.1 %qkv.1 = (f32[1024,128]{1,0:T(8,128)S(1)}, f32[2,2,64,128]{3,2,1,0:T(8,128)S(1)}, bf16[64,512,128]{2,1,0:T(8,128)(2,1)S(1)}, bf16[64,512,128]{2,1,0:T(8,128)(2,1)S(1)}) custom-call(s32[64]{0:T(128)} %pos.3, bf16[64,8192]{1,0:T(8,128)(2,1)} %hid.3, f32[1,8192]{1,0:T(1,128)} %bitcast.9, bf16[8192,2048]{1,0:T(8,128)(2,1)} %wq.1, bf16[8192,256]{1,0:T(8,128)(2,1)} %wk.1, ...), custom_call_target="tpu_custom_call" | custom-call | tf_op jit(solution)/shard_map/qkv/pallas_call | solution.py:529
  13.7 0.0 copy-done
  13.7 7.4 %attention.1 = (bf16[64,512,128]{2,1,0:T(8,128)(2,1)}, bf16[64,512,128]{2,1,0:T(8,128)(2,1)}, f32[1024,128]{1,0:T(8,128)S(1)}, f32[64,128]{1,0:T(8,128)S(1)}, bf...) custom-call(s32[64]{0:T(128)S(1)} %copy-done, ...), custom_call_target="tpu_custom_call", output_to_operand_aliasing={{4}: (3, {}), {5}: (4, {})} | custom-call | tf_op jit(solution)/shard_map/attention/pallas_call | solution.py:555
  21.1 35.8 %output.1 = bf16[64,8192]{1,0:T(8,128)(2,1)S(1)} custom-call(f32[16,64,128]{2,1,0:T(8,128)S(1)} %bitcast.6, f32[64,128]{1,0:T(8,128)S(1)} %get-tuple-element.16.stat, bf16[64,8192]{1,0:T(8,128)(2,1)} %hid.3, bf16[2048,8192]{1,0:T(8,128)(2,1)} %wo.1), custom_call_target="tpu_custom_call" | custom-call | tf_op jit(solution)/shard_map/output/pallas_call | solution.py:580
  56.9 1.0 %copy.17 = bf16[64,8192]{1,0:T(8,128)(2,1)} copy(bf16[64,8192]{1,0:T(8,128)(2,1)S(1)} %output.1) | data formatting | bytes 2097152
Async XLA Ops:
  0.6 13.1 %copy-start = (s32[64]{0:T(128)S(1)}, s32[64]{0:T(128)}, u32[]{:S(2)}) copy-start(s32[64]{0:T(128)} %pos.3) | copy-start | bytes 772

commit v9 on v8

--- a/solution.py
+++ b/solution.py
@@ -13,12 +13,13 @@
 MESH = pl.DeviceIdType.MESH
 F32 = jnp.float32
 BF16 = jnp.bfloat16
-TILES = 4
-BLOCKS = 4
-COUNT = TILES * BLOCKS
-DIRECT = 2
+TILES = 8
+HALVES = 2
+COUNT = TILES * HALVES
+NS = 4
 LAG_Z = 5
 LAG_Y = 5
+DIRECT = 2
 GROUP = 4
 
 
@@ -235,7 +236,8 @@
     heads, batch, hd = acc.shape
     mine = heads // 2
     tile = wob.shape[2]
-    rows_b = batch // BLOCKS
+    rows_s = batch // NS
+    rows_h = batch // HALVES
 
     hcopy = pltpu.make_async_copy(hid, hbuf, lsem.at[TILES])
 
@@ -278,12 +280,12 @@
         pl.semaphore_wait(barrier, 5)
 
     def part_rows(s):
-        return pl.ds(s * rows_b, rows_b)
+        return pl.ds(s * rows_s, rows_s)
 
     st_send = remote(stat, st_p, stsem.at[0], stsem.at[1], partner)
     st_send.start()
     p_send = []
-    for s in range(BLOCKS):
+    for s in range(NS):
         copy = remote(
             acc.at[pl.ds((1 - core) * mine, mine), part_rows(s)], acc_p.at[:, part_rows(s)],
             dsem.at[0, s], dsem.at[1, s], partner,
@@ -309,9 +311,9 @@
     st_c[...] = jnp.where(lane < heads, top, pltpu.roll(total, heads, 1))
     y_send = []
     sty_send = []
-    for s in range(BLOCKS):
+    for s in range(NS):
         p_send[s].wait_recv()
-        sl = slice(s * rows_b, (s + 1) * rows_b)
+        sl = slice(s * rows_s, (s + 1) * rows_s)
         for h in range(mine):
             acc_c[h, sl, :] = acc[core * mine + h, sl, :] * ea[sl, h:h + 1] + acc_p[h, sl, :] * eb[sl, h:h + 1]
         copy = remote(st_c.at[part_rows(s)], st_y.at[part_rows(s)], stsem.at[2], stsem.at[3 + s], ynbr)
@@ -341,11 +343,12 @@
         return remote(tot.at[across, j], tot.at[across, j], fsem.at[5], esem.at[1, j // GROUP], partner)
 
     def project(j):
-        rows = pl.ds(pl.multiple_of((j // TILES) * rows_b, rows_b), rows_b)
-        part[j] = jnp.dot(obf[rows, :], wob[lax.rem(j, TILES)], preferred_element_type=F32)
+        half = j // TILES
+        rows = pl.ds(pl.multiple_of(half * rows_h, rows_h), rows_h)
+        part[j] = jnp.dot(obf[rows, :], wob[j - half * TILES], preferred_element_type=F32)
 
     def values_send(s):
-        sl = slice(s * rows_b, (s + 1) * rows_b)
+        sl = slice(s * rows_s, (s + 1) * rows_s)
         sty_send[s].wait_recv()
         _, ea, eb, total = merge(st_c[sl, :], st_y[sl, :])
         y_send[s].wait_recv()
@@ -359,7 +362,7 @@
         o_send.append(copy)
 
     def values_recv(s):
-        sl = slice(s * rows_b, (s + 1) * rows_b)
+        sl = slice(s * rows_s, (s + 1) * rows_s)
         o_send[s].wait_recv()
         for h in range(mine):
             obf[sl, pl.ds(pl.multiple_of(((1 - core) * mine + h) * hd, hd), hd)] = o_land[h, sl, :].astype(BF16)
@@ -375,31 +378,23 @@
 
         repeat(low, high, tile_step)
 
-    def outer_tiles(low, high):
-        @pl.when(outer)
-        def _():
-            def tile_step(j):
-                project(j)
-                send_a(j).start()
-
-            repeat(low, high, tile_step)
-
     values_send(0)
+    values_send(1)
     values_recv(0)
-    for s in range(BLOCKS):
-        tiles_of = first_tiles if s == 0 else outer_tiles
-        middle = s * TILES + TILES // 2
-        tiles_of(s * TILES, middle)
-        if s < BLOCKS - 1:
-            values_send(s + 1)
-        tiles_of(middle, (s + 1) * TILES)
-        if s < BLOCKS - 1:
-            values_recv(s + 1)
+    values_recv(1)
+    first_tiles(0, TILES // 4)
+    values_send(2)
+    first_tiles(TILES // 4, 3 * TILES // 4)
+    values_send(3)
+    first_tiles(3 * TILES // 4, TILES)
+    values_recv(2)
+    values_recv(3)
     hcopy.wait()
 
     def emit(quarter, j):
-        rows = pl.ds(pl.multiple_of((j // TILES) * rows_b, rows_b), rows_b)
-        where = columns(quarter, lax.rem(j, TILES))
+        half = j // TILES
+        rows = pl.ds(pl.multiple_of(half * rows_h, rows_h), rows_h)
+        where = columns(quarter, j - half * TILES)
         out[rows, where] = (hbuf[rows, where].astype(F32) + tot[quarter, j]).astype(BF16)
 
     def send_x(j):
@@ -431,6 +426,12 @@
 
     @pl.when(outer)
     def _():
+        def second_half(j):
+            project(j)
+            send_a(j).start()
+
+        repeat(TILES, COUNT, second_half)
+
         def step(j):
             @pl.when(j < COUNT)
             def _():
@@ -453,7 +454,7 @@
     @pl.when(inner)
     def _():
         def step(j):
-            @pl.when(j < COUNT - TILES)
+            @pl.when(j < TILES)
             def _():
                 project(TILES + j)
 
@@ -492,7 +493,7 @@
         gather(1, diagonal, g)
     st_send.wait_send()
     remote(st_c, st_y, stsem.at[2], stsem.at[3], ynbr).wait_send()
-    for s in range(BLOCKS):
+    for s in range(NS):
         p_send[s].wait_send()
         y_send[s].wait_send()
         o_send[s].wait_send()
@@ -575,7 +576,7 @@
         ocols = d_model // 4 // TILES
         buf = pltpu.VMEM((mine, batch, hd), F32)
         st = pltpu.VMEM((batch, hd), F32)
-        block = (batch // BLOCKS, ocols)
+        block = (batch // HALVES, ocols)
         chunk = pltpu.VMEM((COUNT,) + block, F32)
         out = pl.pallas_call(
             output_kernel,
@@ -589,8 +590,8 @@
                 buf, buf, buf, buf, buf, st, st, st, chunk, chunk, chunk,
                 pltpu.VMEM((4, COUNT) + block, F32),
                 dma((TILES + 1,)),
-                dma((3 + BLOCKS,)),
-                dma((6, BLOCKS)),
+                dma((3 + NS,)),
+                dma((6, NS)),
                 dma((7,)),
                 dma((4, COUNT)),
                 dma((2, COUNT // GROUP)),

time: 58 us -> 58 us (level)
  no operation moved by 1% of the time
where the time goes in v9:
time: 58 us; the launch traced here: 57.9 us
  Pallas kernels  56.2 us (97%)
  local copies, waits for them, and re-layouts  0.98 us (2%)
  between operations  0.67 us (1%)
    pallas_call x1, Pallas kernels, local_step(): pl.pallas_call(output_kernel, out_shape=pltpu.VMEM((batch, d_model), BF16...  35.7 us
    pallas_call x1, Pallas kernels, local_step(): pl.pallas_call(qkv_kernel, out_shape=(acc_type, pltpu.VMEM((2, 2, batch,...  13.1 us
    pallas_call x1, Pallas kernels, local_step(): pl.pallas_call(attention_kernel, out_shape=(jax.ShapeDtypeStruct(cache, B...  7.39 us

profile of v9, /device:TPU:0, one launch (start us, length us, event | category | flops | bytes accessed | tf_op | source)
XLA Modules:
  0.0 57.9 jit_solution(11049243631745184091)
XLA Ops:
  0.6 0.0 copy-start
  0.6 13.1 %qkv.1 = (f32[1024,128]{1,0:T(8,128)S(1)}, f32[2,2,64,128]{3,2,1,0:T(8,128)S(1)}, bf16[64,512,128]{2,1,0:T(8,128)(2,1)S(1)}, bf16[64,512,128]{2,1,0:T(8,128)(2,1)S(1)}) custom-call(s32[64]{0:T(128)} %pos.3, bf16[64,8192]{1,0:T(8,128)(2,1)} %hid.3, f32[1,8192]{1,0:T(1,128)} %bitcast.9, bf16[8192,2048]{1,0:T(8,128)(2,1)} %wq.1, bf16[8192,256]{1,0:T(8,128)(2,1)} %wk.1, ...), custom_call_target="tpu_custom_call" | custom-call | tf_op jit(solution)/shard_map/qkv/pallas_call | solution.py:530
  13.7 0.0 copy-done
  13.7 7.4 %attention.1 = (bf16[64,512,128]{2,1,0:T(8,128)(2,1)}, bf16[64,512,128]{2,1,0:T(8,128)(2,1)}, f32[1024,128]{1,0:T(8,128)S(1)}, f32[64,128]{1,0:T(8,128)S(1)}, bf...) custom-call(s32[64]{0:T(128)S(1)} %copy-done, ...), custom_call_target="tpu_custom_call", output_to_operand_aliasing={{4}: (3, {}), {5}: (4, {})} | custom-call | tf_op jit(solution)/shard_map/attention/pallas_call | solution.py:556
  21.1 35.7 %output.1 = bf16[64,8192]{1,0:T(8,128)(2,1)S(1)} custom-call(f32[16,64,128]{2,1,0:T(8,128)S(1)} %bitcast.6, f32[64,128]{1,0:T(8,128)S(1)} %get-tuple-element.16.stat, bf16[64,8192]{1,0:T(8,128)(2,1)} %hid.3, bf16[2048,8192]{1,0:T(8,128)(2,1)} %wo.1), custom_call_target="tpu_custom_call" | custom-call | tf_op jit(solution)/shard_map/output/pallas_call | solution.py:581
  56.9 1.0 %copy.17 = bf16[64,8192]{1,0:T(8,128)(2,1)} copy(bf16[64,8192]{1,0:T(8,128)(2,1)S(1)} %output.1) | data formatting | bytes 2097152
Async XLA Ops:
  0.6 13.1 %copy-start = (s32[64]{0:T(128)S(1)}, s32[64]{0:T(128)}, u32[]{:S(2)}) copy-start(s32[64]{0:T(128)} %pos.3) | copy-start | bytes 772

commit v10 on v9

--- a/solution.py
+++ b/solution.py
@@ -19,7 +19,7 @@
 NS = 4
 LAG_Z = 5
 LAG_Y = 5
-DIRECT = 2
+DIRECT = 1
 GROUP = 4
 
 
@@ -122,14 +122,13 @@
     publish(4)
     for t in range(tiles):
         wcopy(t).wait()
-        if t == tiles - 1:
+        if t == tiles // 2:
             for g in range(4):
                 cache_copy(0, g).start()
                 cache_copy(1, g).start()
         q = jnp.dot(rbuf[...], wqb[t], preferred_element_type=F32)
-        for h in range(2):
-            pieces[me, 2 * t + h] = round_bf16(rotate(q[:, h * 128:(h + 1) * 128]))
-            publish(2 * t + h)
+        pieces[me, t] = round_bf16(rotate(q))
+        publish(t)
     for p in order:
         exchange(0, me, p, ynbr).wait_recv()
         exchange(2, across, p, partner).start()
@@ -523,7 +522,7 @@
         d_model, q_cols = w_query.shape
         heads = q_cols // hd
         rows = seq_local * kv_local
-        tiles = 2
+        tiles = 4
         tcols = q_cols // 4 // tiles
         cache = (batch, rows, hd)
         acc_type = pltpu.VMEM((heads * batch, hd), F32)

time: 58 us -> 58.3 us (level)
  no operation moved by 1% of the time
where the time goes in v10:
time: 58.3 us; the launch traced here: 58.2 us
  Pallas kernels  56.5 us (97%)
  local copies, waits for them, and re-layouts  0.98 us (2%)
  between operations  0.67 us (1%)
    pallas_call x1, Pallas kernels, local_step(): pl.pallas_call(output_kernel, out_shape=pltpu.VMEM((batch, d_model), BF16...  36.1 us
    pallas_call x1, Pallas kernels, local_step(): pl.pallas_call(qkv_kernel, out_shape=(acc_type, pltpu.VMEM((2, 2, batch,...  13.1 us
    pallas_call x1, Pallas kernels, local_step(): pl.pallas_call(attention_kernel, out_shape=(jax.ShapeDtypeStruct(cache, B...  7.39 us

profile of v10, /device:TPU:0, one launch (start us, length us, event | category | flops | bytes accessed | tf_op | source)
XLA Modules:
  0.0 58.2 jit_solution(1047304505757049554)
XLA Ops:
  0.6 0.0 copy-start
  0.6 13.1 %qkv.1 = (f32[1024,128]{1,0:T(8,128)S(1)}, f32[2,2,64,128]{3,2,1,0:T(8,128)S(1)}, bf16[64,512,128]{2,1,0:T(8,128)(2,1)S(1)}, bf16[64,512,128]{2,1,0:T(8,128)(2,1)S(1)}) custom-call(s32[64]{0:T(128)} %pos.3, bf16[64,8192]{1,0:T(8,128)(2,1)} %hid.3, f32[1,8192]{1,0:T(1,128)} %bitcast.9, bf16[8192,2048]{1,0:T(8,128)(2,1)} %wq.1, bf16[8192,256]{1,0:T(8,128)(2,1)} %wk.1, ...), custom_call_target="tpu_custom_call" | custom-call | tf_op jit(solution)/shard_map/qkv/pallas_call | solution.py:529
  13.7 0.0 copy-done
  13.7 7.4 %attention.1 = (bf16[64,512,128]{2,1,0:T(8,128)(2,1)}, bf16[64,512,128]{2,1,0:T(8,128)(2,1)}, f32[1024,128]{1,0:T(8,128)S(1)}, f32[64,128]{1,0:T(8,128)S(1)}, bf...) custom-call(s32[64]{0:T(128)S(1)} %copy-done, ...), custom_call_target="tpu_custom_call", output_to_operand_aliasing={{4}: (3, {}), {5}: (4, {})} | custom-call | tf_op jit(solution)/shard_map/attention/pallas_call | solution.py:555
  21.1 36.1 %output.1 = bf16[64,8192]{1,0:T(8,128)(2,1)S(1)} custom-call(f32[16,64,128]{2,1,0:T(8,128)S(1)} %bitcast.6, f32[64,128]{1,0:T(8,128)S(1)} %get-tuple-element.16.stat, bf16[64,8192]{1,0:T(8,128)(2,1)} %hid.3, bf16[2048,8192]{1,0:T(8,128)(2,1)} %wo.1), custom_call_target="tpu_custom_call" | custom-call | tf_op jit(solution)/shard_map/output/pallas_call | solution.py:580
  57.2 1.0 %copy.17 = bf16[64,8192]{1,0:T(8,128)(2,1)} copy(bf16[64,8192]{1,0:T(8,128)(2,1)S(1)} %output.1) | data formatting | bytes 2097152
Async XLA Ops:
  0.6 13.1 %copy-start = (s32[64]{0:T(128)S(1)}, s32[64]{0:T(128)}, u32[]{:S(2)}) copy-start(s32[64]{0:T(128)} %pos.3) | copy-start | bytes 772

commit v11 on v9

--- a/solution.py
+++ b/solution.py
@@ -19,7 +19,6 @@
 NS = 4
 LAG_Z = 5
 LAG_Y = 5
-DIRECT = 2
 GROUP = 4
 
 
@@ -271,13 +270,11 @@
 
     @pl.when(outer)
     def _():
-        pl.semaphore_signal(barrier, inc=1, device_id={"sp": across, "tp": z_in}, device_id_type=MESH)
+        pl.semaphore_wait(barrier, 3)
+
+    @pl.when(inner)
+    def _():
         pl.semaphore_wait(barrier, 4)
-
-    @pl.when(inner)
-    def _():
-        pl.semaphore_signal(barrier, inc=1, device_id={"sp": across, "tp": z_out}, device_id_type=MESH)
-        pl.semaphore_wait(barrier, 5)
 
     def part_rows(s):
         return pl.ds(s * rows_s, rows_s)
@@ -397,10 +394,8 @@
         where = columns(quarter, j - half * TILES)
         out[rows, where] = (hbuf[rows, where].astype(F32) + tot[quarter, j]).astype(BF16)
 
-    def send_x(j):
-        return remote(tot.at[me, j], tot.at[me, j], fsem.at[6], rsem.at[3, j], {"sp": across, "tp": z_out})
-
     def share(j):
+        send_d(j).start()
         send_e(j).start()
         emit(me, j)
 
@@ -436,11 +431,6 @@
             @pl.when(j < COUNT)
             def _():
                 send_c(j).wait_recv()
-
-                @pl.when(j < COUNT - DIRECT)
-                def _():
-                    send_d(j).start()
-
                 share(j)
 
             collect(j - LAG_Y)
@@ -448,8 +438,6 @@
 
         repeat(0, COUNT + LAG_Y, step)
         remote(part, land_a, fsem.at[0], rsem.at[0, 0], {"tp": z_in}).wait_send()
-        sent = tot.at[me, pl.ds(0, COUNT - DIRECT)]
-        remote(sent, sent, fsem.at[3], rsem.at[3, 0], ynbr).wait_send()
 
     @pl.when(inner)
     def _():
@@ -471,12 +459,6 @@
                 send_b(k).wait_recv()
                 tot[me, k] = part[k] + land_b[k]
                 send_c(k).start()
-                send_d(k).start()
-
-                @pl.when(k >= COUNT - DIRECT)
-                def _():
-                    send_x(k).start()
-
                 share(k)
 
             collect(k - LAG_Y)
@@ -485,9 +467,6 @@
         repeat(0, COUNT + LAG_Z + LAG_Y, step)
         remote(part, land_b, fsem.at[1], rsem.at[1, 0], {"tp": z_in}).wait_send()
         remote(tot.at[me], tot.at[me], fsem.at[2], rsem.at[2, 0], {"tp": z_out}).wait_send()
-        remote(tot.at[me], tot.at[me], fsem.at[3], rsem.at[3, 0], ynbr).wait_send()
-        sent = tot.at[me, pl.ds(0, DIRECT)]
-        remote(sent, sent, fsem.at[6], rsem.at[3, 0], ynbr).wait_send()
 
     for g in range(groups):
         gather(1, diagonal, g)
@@ -497,6 +476,7 @@
         p_send[s].wait_send()
         y_send[s].wait_send()
         o_send[s].wait_send()
+    remote(tot.at[me], tot.at[me], fsem.at[3], rsem.at[3, 0], ynbr).wait_send()
     remote(tot.at[me], tot.at[me], fsem.at[4], esem.at[0, 0], partner).wait_send()
     remote(tot.at[across], tot.at[across], fsem.at[5], esem.at[1, 0], partner).wait_send()
 
@@ -592,7 +572,7 @@
                 dma((TILES + 1,)),
                 dma((3 + NS,)),
                 dma((6, NS)),
-                dma((7,)),
+                dma((6,)),
                 dma((4, COUNT)),
                 dma((2, COUNT // GROUP)),
             ],

time: 58 us -> 57.4 us (0.990)
  Pallas kernels: 56.2 us -> 55.6 us
    pallas_call x1, Pallas kernels: 35.7 us -> 35.1 us  [local_step(): pl.pallas_call(output_kernel, out_shape=pltpu.VMEM((batch, d_model), BF16...]
where the time goes in v11:
time: 57.4 us; the launch traced here: 57.2 us
  Pallas kernels  55.6 us (97%)
  local copies, waits for them, and re-layouts  0.98 us (2%)
  between operations  0.67 us (1%)
    pallas_call x1, Pallas kernels, local_step(): pl.pallas_call(output_kernel, out_shape=pltpu.VMEM((batch, d_model), BF16...  35.1 us
    pallas_call x1, Pallas kernels, local_step(): pl.pallas_call(qkv_kernel, out_shape=(acc_type, pltpu.VMEM((2, 2, batch,...  13.1 us
    pallas_call x1, Pallas kernels, local_step(): pl.pallas_call(attention_kernel, out_shape=(jax.ShapeDtypeStruct(cache, B...  7.39 us

profile of v11, /device:TPU:0, one launch (start us, length us, event | category | flops | bytes accessed | tf_op | source)
XLA Modules:
  0.0 57.2 jit_solution(9214989944991535416)
XLA Ops:
  0.6 0.0 copy-start
  0.6 13.1 %qkv.1 = (f32[1024,128]{1,0:T(8,128)S(1)}, f32[2,2,64,128]{3,2,1,0:T(8,128)S(1)}, bf16[64,512,128]{2,1,0:T(8,128)(2,1)S(1)}, bf16[64,512,128]{2,1,0:T(8,128)(2,1)S(1)}) custom-call(s32[64]{0:T(128)} %pos.3, bf16[64,8192]{1,0:T(8,128)(2,1)} %hid.3, f32[1,8192]{1,0:T(1,128)} %bitcast.9, bf16[8192,2048]{1,0:T(8,128)(2,1)} %wq.1, bf16[8192,256]{1,0:T(8,128)(2,1)} %wk.1, ...), custom_call_target="tpu_custom_call" | custom-call | tf_op jit(solution)/shard_map/qkv/pallas_call | solution.py:510
  13.7 0.0 copy-done
  13.7 7.4 %attention.1 = (bf16[64,512,128]{2,1,0:T(8,128)(2,1)}, bf16[64,512,128]{2,1,0:T(8,128)(2,1)}, f32[1024,128]{1,0:T(8,128)S(1)}, f32[64,128]{1,0:T(8,128)S(1)}, bf...) custom-call(s32[64]{0:T(128)S(1)} %copy-done, ...), custom_call_target="tpu_custom_call", output_to_operand_aliasing={{4}: (3, {}), {5}: (4, {})} | custom-call | tf_op jit(solution)/shard_map/attention/pallas_call | solution.py:536
  21.1 35.1 %output.1 = bf16[64,8192]{1,0:T(8,128)(2,1)S(1)} custom-call(f32[16,64,128]{2,1,0:T(8,128)S(1)} %bitcast.6, f32[64,128]{1,0:T(8,128)S(1)} %get-tuple-element.16.stat, bf16[64,8192]{1,0:T(8,128)(2,1)} %hid.3, bf16[2048,8192]{1,0:T(8,128)(2,1)} %wo.1), custom_call_target="tpu_custom_call" | custom-call | tf_op jit(solution)/shard_map/output/pallas_call | solution.py:561
  56.3 1.0 %copy.17 = bf16[64,8192]{1,0:T(8,128)(2,1)} copy(bf16[64,8192]{1,0:T(8,128)(2,1)S(1)} %output.1) | data formatting | bytes 2097152
Async XLA Ops:
  0.6 13.1 %copy-start = (s32[64]{0:T(128)S(1)}, s32[64]{0:T(128)}, u32[]{:S(2)}) copy-start(s32[64]{0:T(128)} %pos.3) | copy-start | bytes 772
